TPU v7x, 32 devices: a whole 2x2x4 slice. The times are simulated.
32 devices in a mesh: data: 4 (over z), stage: 8 (over y, x, core).
Axes of the slice: x: 2, y: 2, z: 4, core: 2. Of those that a mesh axis runs over, the one named last changes fastest.
Arguments:
- act_in: bfloat16 [24, 128, 16, 256], P(None, 'data')
- cot_out: bfloat16 [24, 128, 16, 256], P(None, 'data')
- w_gate: bfloat16 [2, 8, 256, 1024], P(None, 'stage', 'data')
- w_in: bfloat16 [2, 8, 256, 1024], P(None, 'stage', 'data')
- w_out: bfloat16 [2, 8, 1024, 256], P(None, 'stage', 'data')
Outputs:
- output 1: bfloat16 [24, 128, 16, 256], P(None, 'data')
- output 2: float32 [2, 8, 256, 1024], P(None, 'stage', 'data')
- output 3: float32 [2, 8, 256, 1024], P(None, 'stage', 'data')
- output 4: float32 [2, 8, 1024, 256], P(None, 'stage', 'data')
All inputs are finite; a program needn't handle non-finite values.
Results may differ from a plain program's by a relative error of at most 0.02.
Values are sent between devices in bfloat16 or wider.
A program may use at most 1 GiB of HBM per device.

v0:
```python
import jax
import jax.numpy as jnp
from jax import lax
from jax.sharding import PartitionSpec as P

NORM_EPS = 1e-6


def contract_rows(left, right):
    return lax.dot_general(left, right, (((0,), (0,)), ((), ())), preferred_element_type=jnp.float32)


def contract_cols(left, right):
    return lax.dot_general(left, right, (((1,), (1,)), ((), ())), preferred_element_type=jnp.float32)


def pick_at(stack, index):
    return lax.dynamic_index_in_dim(stack, index, keepdims=False)


def layer_forward(rows_in, gate_w, lin_w, proj_w):
    rows_f32 = rows_in.astype(jnp.float32)
    inv_rms = lax.rsqrt(jnp.mean(rows_f32 * rows_f32, axis=-1, keepdims=True) + NORM_EPS)
    normed = (rows_f32 * inv_rms).astype(jnp.bfloat16)
    gate_pre = jnp.dot(normed, gate_w, preferred_element_type=jnp.float32)
    lin_pre = jnp.dot(normed, lin_w, preferred_element_type=jnp.float32)
    gate_act = gate_pre * jax.nn.sigmoid(gate_pre)
    hidden = (gate_act * lin_pre).astype(jnp.bfloat16)
    proj_out = jnp.dot(hidden, proj_w, preferred_element_type=jnp.float32)
    return (rows_f32 + proj_out).astype(jnp.bfloat16)


def layer_backward(rows_in, grad_rows, gate_w, lin_w, proj_w):
    rows_f32 = rows_in.astype(jnp.float32)
    inv_rms = lax.rsqrt(jnp.mean(rows_f32 * rows_f32, axis=-1, keepdims=True) + NORM_EPS)
    scaled = rows_f32 * inv_rms
    normed = scaled.astype(jnp.bfloat16)
    gate_pre = jnp.dot(normed, gate_w, preferred_element_type=jnp.float32)
    lin_pre = jnp.dot(normed, lin_w, preferred_element_type=jnp.float32)
    gate_sig = jax.nn.sigmoid(gate_pre)
    gate_act = gate_pre * gate_sig
    hidden = (gate_act * lin_pre).astype(jnp.bfloat16)
    grad_proj = contract_rows(hidden, grad_rows)
    grad_hidden = contract_cols(grad_rows, proj_w)
    d_gate = (grad_hidden * lin_pre * gate_sig * (1.0 + gate_pre * (1.0 - gate_sig))).astype(jnp.bfloat16)
    d_lin = (grad_hidden * gate_act).astype(jnp.bfloat16)
    grad_gate = contract_rows(normed, d_gate)
    grad_lin = contract_rows(normed, d_lin)
    grad_norm = contract_cols(d_gate, gate_w) + contract_cols(d_lin, lin_w)
    grad_in = grad_rows.astype(jnp.float32) + inv_rms * (grad_norm - scaled * jnp.mean(grad_norm * scaled, axis=-1, keepdims=True))
    return grad_in.astype(jnp.bfloat16), grad_gate, grad_lin, grad_proj


def solution(mesh):
    stage_n = mesh.shape["stage"]
    fwd_perm = [(src, (src + 1) % stage_n) for src in range(stage_n)]
    bwd_perm = [(src, (src - 1) % stage_n) for src in range(stage_n)]
    act_spec = P(None, "data", None, None)
    w_spec = P(None, "stage", "data", None)

    def body(act_in, cot_out, w_gate, w_in, w_out):
        n_micro, rows_dev, seq_len, dmodel = act_in.shape
        ffn_dim = w_gate.shape[3]
        tok_rows = rows_dev * seq_len
        act_micro = act_in.reshape(n_micro, tok_rows, dmodel)
        cot_micro = cot_out.reshape(n_micro, tok_rows, dmodel)
        gate_full = lax.all_gather(w_gate[:, 0], "data", axis=1, tiled=True)
        lin_full = lax.all_gather(w_in[:, 0], "data", axis=1, tiled=True)
        proj_full = lax.all_gather(w_out[:, 0], "data", axis=1, tiled=True)
        stage_idx = lax.axis_index("stage")
        n_steps = 2 * n_micro
        round_len = 2 * stage_n
        tick_ids = jnp.arange(n_steps + stage_n - 1)

        def fwd_tick(recv_rows, tick_idx):
            step_idx = jnp.clip(tick_idx - stage_idx, 0, n_steps - 1)
            virt_idx = (step_idx % round_len) // stage_n
            micro_idx = (step_idx // round_len) * stage_n + step_idx % stage_n
            layer_in = jnp.where((virt_idx == 0) & (stage_idx == 0), pick_at(act_micro, micro_idx), recv_rows)
            layer_out = layer_forward(layer_in, pick_at(gate_full, virt_idx), pick_at(lin_full, virt_idx), pick_at(proj_full, virt_idx))
            return lax.ppermute(layer_out, "stage", fwd_perm), layer_in

        zero_rows = jnp.zeros((tok_rows, dmodel), jnp.bfloat16)
        last_fwd, seen_in = lax.scan(fwd_tick, zero_rows, tick_ids)
        saved_in = lax.dynamic_slice_in_dim(seen_in, stage_idx, n_steps, axis=0)

        def bwd_tick(carry_in, tick_idx):
            recv_rows, acc_gate, acc_lin, acc_proj = carry_in
            raw_step = tick_idx - (stage_n - 1 - stage_idx)
            is_valid = (raw_step >= 0) & (raw_step < n_steps)
            step_idx = jnp.clip(raw_step, 0, n_steps - 1)
            group_idx = step_idx // round_len
            within = step_idx % round_len
            virt_idx = 1 - within // stage_n
            slot_idx = within % stage_n
            micro_idx = group_idx * stage_n + slot_idx
            fwd_pos = group_idx * round_len + virt_idx * stage_n + slot_idx
            grad_out = jnp.where((virt_idx == 1) & (stage_idx == stage_n - 1), pick_at(cot_micro, micro_idx), recv_rows)
            grad_out = jnp.where(is_valid, grad_out, jnp.zeros_like(grad_out))
            grad_in, grad_g, grad_l, grad_p = layer_backward(pick_at(saved_in, fwd_pos), grad_out, pick_at(gate_full, virt_idx), pick_at(lin_full, virt_idx), pick_at(proj_full, virt_idx))
            acc_gate = lax.dynamic_update_index_in_dim(acc_gate, pick_at(acc_gate, virt_idx) + grad_g, virt_idx, 0)
            acc_lin = lax.dynamic_update_index_in_dim(acc_lin, pick_at(acc_lin, virt_idx) + grad_l, virt_idx, 0)
            acc_proj = lax.dynamic_update_index_in_dim(acc_proj, pick_at(acc_proj, virt_idx) + grad_p, virt_idx, 0)
            return (lax.ppermute(grad_in, "stage", bwd_perm), acc_gate, acc_lin, acc_proj), grad_in

        zero_up = jnp.zeros((2, dmodel, ffn_dim), jnp.float32)
        zero_down = jnp.zeros((2, ffn_dim, dmodel), jnp.float32)
        carry_out, seen_grad = lax.scan(bwd_tick, (zero_rows, zero_up, zero_up, zero_down), tick_ids)
        first_grad = seen_grad[stage_n - 1:stage_n - 1 + n_steps].reshape(n_micro // stage_n, 2, stage_n, tok_rows, dmodel)[:, 1]
        first_grad = jnp.where(stage_idx == 0, first_grad, jnp.zeros_like(first_grad))
        grad_act = lax.psum(first_grad, "stage").reshape(n_micro, rows_dev, seq_len, dmodel)
        grad_gate = lax.psum_scatter(carry_out[1], "data", scatter_dimension=1, tiled=True)[:, None]
        grad_lin = lax.psum_scatter(carry_out[2], "data", scatter_dimension=1, tiled=True)[:, None]
        grad_proj = lax.psum_scatter(carry_out[3], "data", scatter_dimension=1, tiled=True)[:, None]
        return grad_act, grad_gate, grad_lin, grad_proj

    return jax.shard_map(body, mesh=mesh, in_specs=(act_spec, act_spec, w_spec, w_spec, w_spec), out_specs=(act_spec, w_spec, w_spec, w_spec), check_vma=False)
```

profile of v0, /device:TPU:0, one launch (start us, length us, event | category | flops | bytes accessed | tf_op | source)
XLA Modules:
  0.0 2643.1 jit_solution(9825190630799537306)
XLA Ops:
  9.4 30.8 %all-gather.7.cloned.1.call-done = bf16[2,1,256,1024]{3,2,0,1:T(8,128)(2,1)} async-done(((bf16[2,1,64,1024]{3,2,0,1:T(8,128)(2,1)}), bf16[2,1,256,1024]{3,2,0,1:T(8,128)(2,1)}) %all-gather.7.cloned.1.call-update) | async-done | bytes 1048592 | tf_op jit(solution)/shard_map/all_gather | solution.py:67
  40.2 28.9 %all-gather.9.cloned.1.call-done = bf16[2,1,256,1024]{3,2,0,1:T(8,128)(2,1)} async-done(((bf16[2,1,64,1024]{3,2,0,1:T(8,128)(2,1)}), bf16[2,1,256,1024]{3,2,0,1:T(8,128)(2,1)}) %all-gather.9.cloned.1.call-update) | async-done | bytes 1048592 | tf_op jit(solution)/shard_map/all_gather | solution.py:68
  69.1 28.9 %all-gather.11.cloned.1.call-done = bf16[2,1,1024,256]{3,2,0,1:T(8,128)(2,1)} async-done(((bf16[2,1,256,256]{3,2,0,1:T(8,128)(2,1)}), bf16[2,1,1024,256]{3,2,0,1:T(8,128)(2,1)}) %all-gather.11.cloned.1.call-update) | async-done | bytes 1048592 | tf_op jit(solution)/shard_map/all_gather | solution.py:69
  98.7 6.9 broadcast.110.clone.1
  105.6 682.6 %while.36 = (s32[]{:T(128)}, bf16[512,256]{1,0:T(8,128)(2,1)}, bf16[55,512,256]{1,2,0:T(8,128)(2,1)}, s32[55]{0:T(128)S(1)}, s32[]{:T(128)}, /*index=5*/pred[]{:...) while((s32[]{:T(128)}, bf16[512,256]{1,0:T(8,128)(2,1)}, ...), condition=%wide.region_2.3_spmd, body=%wide.region_0.2_spmd.sunk | while | flops 810156544 | bytes 9711325 | solution.py:84
  112.1 5.8 collective-permute-done
  124.5 5.8 collective-permute-done
  174.0 5.8 collective-permute-done
  211.2 5.8 collective-permute-done
  223.6 5.8 collective-permute-done
  261.0 5.8 collective-permute-done
  273.4 5.8 collective-permute-done
  285.8 5.8 collective-permute-done
  298.3 5.8 collective-permute-done
  310.6 5.8 collective-permute-done
  323.0 5.8 collective-permute-done
  347.8 5.8 collective-permute-done
  372.5 5.8 collective-permute-done
  397.2 5.8 collective-permute-done
  409.7 5.8 collective-permute-done
  447.0 5.8 collective-permute-done
  459.4 5.8 collective-permute-done
  471.9 5.8 collective-permute-done
  496.8 5.8 collective-permute-done
  509.2 5.8 collective-permute-done
  546.3 5.8 collective-permute-done
  633.1 5.8 collective-permute-done
  645.5 5.8 collective-permute-done
  658.0 5.8 collective-permute-done
  670.4 5.8 collective-permute-done
  695.3 5.8 collective-permute-done
  707.8 5.8 collective-permute-done
  732.6 5.8 collective-permute-done
  745.1 5.8 collective-permute-done
  757.5 5.8 collective-permute-done
  770.0 5.8 collective-permute-done
  782.4 5.8 collective-permute-done
  788.2 10.5 constant_dynamic-slice_fusion.4
  804.1 6.9 broadcast.110
  810.9 1555.6 %while.37 = (s32[]{:T(128)}, bf16[512,256]{0,1:T(8,128)(2,1)}, f32[2,256,1024]{2,1,0:T(8,128)}, f32[2,256,1024]{2,1,0:T(8,128)}, f32[2,1024,256]{2,1,0:T(8,128)}...) while((s32[]{:T(128)}, bf16[512,256]{0,1:T(8,128)(2,1)}, ...), condition=%wide.region_6.7_spmd, body=%wide.region_3.6_spmd.sunk | while | flops 2162164224 | bytes 84176408 | solution.py:108
  2366.5 6.3 slice.6
  2376.2 8.6 copy.28
  2384.8 5.9 broadcast_select_fusion
  2392.7 99.3 %all-reduce.2.cloned.1.call-done = bf16[24,32,16,256]{3,2,1,0:T(8,128)(2,1)} async-done(((bf16[24,32,16,256]{3,2,1,0:T(8,128)(2,1)}), bf16[24,32,16,256]{3,2,1,0:T(8,128)(2,1)}) %all-reduce.2.cloned.1.call-update) | async-done | bytes 6291472 | tf_op jit(solution)/shard_map/psum | solution.py:111
  2491.9 46.8 %reduce-scatter.8.cloned.1.call-done = f32[2,256,256]{2,1,0:T(8,128)} async-done(((f32[2,1024,256]{2,1,0:T(8,128)}), f32[2,256,256]{2,1,0:T(8,128)}) %reduce-scatter.8.cloned.1.call-update) | async-done | bytes 524304 | tf_op jit(solution)/shard_map/reduce_scatter | solution.py:114
  2538.7 45.7 %reduce-scatter.4.cloned.1.call-done = f32[2,64,1024]{2,1,0:T(8,128)} async-done(((f32[2,256,1024]{2,1,0:T(8,128)}), f32[2,64,1024]{2,1,0:T(8,128)}) %reduce-scatter.4.cloned.1.call-update) | async-done | bytes 524304 | tf_op jit(solution)/shard_map/reduce_scatter | solution.py:112
  2584.4 45.8 %reduce-scatter.6.cloned.1.call-done = f32[2,64,1024]{2,1,0:T(8,128)} async-done(((f32[2,256,1024]{2,1,0:T(8,128)}), f32[2,64,1024]{2,1,0:T(8,128)}) %reduce-scatter.6.cloned.1.call-update) | async-done | bytes 524304 | tf_op jit(solution)/shard_map/reduce_scatter | solution.py:113
  2630.1 6.1 copy.66
  (2137 shorter events, 1981.5 us)
Async XLA Ops:
  7.2 33.1 %all-gather.7.cloned.1.call-start = ((), (), s32[]{:S(2)}) async-start(), calls=%async_computation.7 | async-start | bytes 1310720 | tf_op jit(solution)/shard_map/all_gather | solution.py:67
  7.9 61.2 %all-gather.9.cloned.1.call-start = ((), (), s32[]{:S(2)}) async-start(), calls=%async_computation.8 | async-start | bytes 1310720 | tf_op jit(solution)/shard_map/all_gather | solution.py:68
  8.6 89.3 %all-gather.11.cloned.1.call-start = ((), (), s32[]{:S(2)}) async-start(), calls=%async_computation.9 | async-start | bytes 1310720 | tf_op jit(solution)/shard_map/all_gather | solution.py:69
  9.4 2482.5 %all-reduce.2.cloned.1.call-start = ((), (), s32[]{:S(2)}) async-start(), calls=%async_computation.3 | async-start | bytes 12582912 | tf_op jit(solution)/shard_map/psum | solution.py:111
  911.5 12.8 collective-permute-start.1
  943.2 8.7 collective-permute-start.1
  998.6 8.7 collective-permute-start.1
  1026.3 9.1 collective-permute-start.1
  1054.3 9.7 collective-permute-start.1
  1138.3 12.7 collective-permute-start.1
  1169.9 8.7 collective-permute-start.1
  1252.9 9.0 collective-permute-start.1
  1280.9 8.7 collective-permute-start.1
  1336.2 8.8 collective-permute-start.1
  1363.9 12.7 collective-permute-start.1
  1395.6 8.8 collective-permute-start.1
  1423.3 8.7 collective-permute-start.1
  1478.6 9.1 collective-permute-start.1
  1506.6 9.7 collective-permute-start.1
  1562.9 8.8 collective-permute-start.1
  1590.6 12.7 collective-permute-start.1
  1622.2 8.7 collective-permute-start.1
  1649.9 8.7 collective-permute-start.1
  1677.6 8.7 collective-permute-start.1
  1705.2 9.0 collective-permute-start.1
  1733.2 8.7 collective-permute-start.1
  1760.9 8.7 collective-permute-start.1
  1788.6 8.8 collective-permute-start.1
  1816.3 12.6 collective-permute-start.1
  1847.9 8.7 collective-permute-start.1
  1875.6 8.7 collective-permute-start.1
  1903.3 8.8 collective-permute-start.1
  1931.0 9.0 collective-permute-start.1
  1959.0 9.7 collective-permute-start.1
  1987.6 8.7 collective-permute-start.1
  2015.2 8.8 collective-permute-start.1
  2043.0 12.6 collective-permute-start.1
  2074.6 8.7 collective-permute-start.1
  2129.9 8.7 collective-permute-start.1
  2157.6 9.0 collective-permute-start.1
  2185.5 9.7 collective-permute-start.1
  2241.8 8.8 collective-permute-start.1
  2269.6 12.6 collective-permute-start.1
  2301.1 8.7 collective-permute-start.1
  2356.4 8.7 collective-permute-start.1
  2390.7 148.0 %reduce-scatter.8.cloned.1.call-start = ((), (), s32[]{:S(2)}) async-start(), calls=%async_computation.6 | async-start | bytes 2621440 | tf_op jit(solution)/shard_map/reduce_scatter | solution.py:114
  2391.3 193.0 %reduce-scatter.4.cloned.1.call-start = ((), (), s32[]{:S(2)}) async-start(), calls=%async_computation.4 | async-start | bytes 2621440 | tf_op jit(solution)/shard_map/reduce_scatter | solution.py:112
  2391.9 238.2 %reduce-scatter.6.cloned.1.call-start = ((), (), s32[]{:S(2)}) async-start(), calls=%async_computation.5 | async-start | bytes 2621440 | tf_op jit(solution)/shard_map/reduce_scatter | solution.py:113
  (345 other events, 1155.1 us)
Sparse Core Ops, SparseCore 0:
  9.5 30.6 all-gather.6
  41.8 27.2 all-gather.8
  70.7 27.2 all-gather.10
  2390.9 101.0 all-reduce.1
  2494.6 44.0 reduce-scatter.7
  2541.4 42.8 reduce-scatter.3
  2587.2 42.8 reduce-scatter.5
where the time goes:
time: 2660 us; the launch traced here: 2640 us
  matrix products  1150 us (43%)
  waiting for transfers between devices  650 us (24%)
  local copies, waits for them, and re-layouts  419 us (16%)
  other arithmetic  286 us (11%)
  loops' own time  83.9 us (3%)
  starting transfers between devices  35.1 us (1%)
    dot_general x165, matrix products, contract_rows(): lax.dot_general(left, right, (((0,), (0,)), ((), ())), preferred_element_...  358 us
    ppermute x55, waiting for transfers between devices, fwd_tick(): return (lax.ppermute(layer_out, 'stage', fwd_perm), layer_in)  320 us
    dot_general x165, matrix products, contract_cols(): lax.dot_general(left, right, (((1,), (1,)), ((), ())), preferred_element_...  308 us
    dot_general x55, matrix products, layer_backward(): lin_pre = jnp.dot(normed, lin_w, preferred_element_type=jnp.float32)  160 us
    dynamic_slice x220, local copies, waits for them, and re-layouts, pick_at(): return lax.dynamic_index_in_dim(stack, index, keepdims=False)  153 us
    dot_general x55, matrix products, layer_forward(): proj_out = jnp.dot(hidden, proj_w, preferred_element_type=jnp.float32)  152 us
    dot_general x55, matrix products, layer_backward(): gate_pre = jnp.dot(normed, gate_w, preferred_element_type=jnp.float32)  150 us
    dynamic_update_slice x55, other arithmetic, body(): last_fwd, seen_in = lax.scan(fwd_tick, zero_rows, tick_ids)  104 us
  transfers between devices with their start and end apart: 117, of which 62 were waited for; matrix products, arithmetic and copies ran while one was open for 19% of the time, Pallas kernels for 0%

commit v1 on v0

v1 whole, which is shorter than its diff:
```python
import jax
import jax.numpy as jnp
from jax import lax
from jax.sharding import PartitionSpec as P

NORM_EPS = 1e-6
GRP = ("stage", "data")


def dot_rows(left, right):
    return lax.dot_general(left, right, (((0,), (0,)), ((), ())), preferred_element_type=jnp.float32)


def dot_cols(left, right):
    return lax.dot_general(left, right, (((1,), (1,)), ((), ())), preferred_element_type=jnp.float32)


def dot_f32(left, right):
    return jnp.dot(left, right, preferred_element_type=jnp.float32)


def block_forward(rows, gate_w, lin_w, proj_w):
    h = rows.astype(jnp.float32)
    r = lax.rsqrt(jnp.mean(h * h, axis=-1, keepdims=True) + NORM_EPS)
    n = (h * r).astype(jnp.bfloat16)
    a = dot_f32(n, gate_w)
    b = dot_f32(n, lin_w)
    u = (a * jax.nn.sigmoid(a) * b).astype(jnp.bfloat16)
    return (h + dot_f32(u, proj_w)).astype(jnp.bfloat16)


def block_backward(rows, e, gate_w, lin_w, proj_w):
    h = rows.astype(jnp.float32)
    r = lax.rsqrt(jnp.mean(h * h, axis=-1, keepdims=True) + NORM_EPS)
    hr = h * r
    n = hr.astype(jnp.bfloat16)
    a = dot_f32(n, gate_w)
    b = dot_f32(n, lin_w)
    s = jax.nn.sigmoid(a)
    act = a * s
    u = (act * b).astype(jnp.bfloat16)
    d_out = dot_rows(u, e)
    t = dot_cols(e, proj_w)
    da = (t * b * s * (1.0 + a * (1.0 - s))).astype(jnp.bfloat16)
    db = (t * act).astype(jnp.bfloat16)
    d_gate = dot_rows(n, da)
    d_in = dot_rows(n, db)
    q = dot_cols(da, gate_w) + dot_cols(db, lin_w)
    g = e.astype(jnp.float32) + r * (q - hr * jnp.mean(q * hr, axis=-1, keepdims=True))
    return g.astype(jnp.bfloat16), d_gate, d_in, d_out


def solution(mesh):
    n_stage = mesh.shape["stage"]
    act_spec = P(None, "data", None, None)
    w_spec = P(None, "stage", "data", None)

    def body(act_in, cot_out, w_gate, w_in, w_out):
        n_micro, n_seq, n_tok, width = act_in.shape
        n_v = w_gate.shape[0]
        own = n_micro // n_stage
        stage = lax.axis_index("stage")
        h = lax.dynamic_slice_in_dim(act_in, stage * own, own, 0).reshape(-1, width)
        e = lax.dynamic_slice_in_dim(cot_out, stage * own, own, 0).reshape(-1, width)

        def whole(w, v):
            full = lax.all_gather(w[v, 0], GRP, axis=0, tiled=True)
            return full.reshape(n_stage, -1, w.shape[3])

        weights = [tuple(whole(w, v) for w in (w_gate, w_in, w_out)) for v in range(n_v)]
        saved = []
        for v in range(n_v):
            for p in range(n_stage):
                saved.append(h)
                h = block_forward(h, *(w[p] for w in weights[v]))
        grads = [None] * n_v
        for v in reversed(range(n_v)):
            parts = [None] * n_stage
            for p in reversed(range(n_stage)):
                e, *parts[p] = block_backward(saved[v * n_stage + p], e, *(w[p] for w in weights[v]))
            grads[v] = []
            for k in range(3):
                stacked = jnp.concatenate([parts[p][k] for p in range(n_stage)], axis=0)
                grads[v].append(lax.psum_scatter(stacked, GRP, scatter_dimension=0, tiled=True))
        grad_act = lax.all_gather(e.reshape(own, n_seq, n_tok, width), "stage", axis=0, tiled=True)
        outs = [jnp.stack([grads[v][k] for v in range(n_v)])[:, None] for k in range(3)]
        return grad_act, *outs

    return jax.shard_map(body, mesh=mesh, in_specs=(act_spec, act_spec, w_spec, w_spec, w_spec), out_specs=(act_spec, w_spec, w_spec, w_spec), check_vma=False)
```

time: 2660 us -> 1860 us (0.70)
  matrix products: 1150 us -> 443 us
  waiting for transfers between devices: 650 us -> 1300 us
  local copies, waits for them, and re-layouts: 419 us -> 62.5 us
  other arithmetic: 286 us -> 24.2 us
  loops' own time: 83.9 us -> 0 us
  starting transfers between devices: 35.1 us -> 1.86 us
    reduce_scatter x3 -> x6, waiting for transfers between devices: 138 us -> 1030 us  [body(): lax.psum_scatter(stacked, GRP, scatter_dimension=0, tiled=True)]
    dot_general x550 -> x143, matrix products: 1150 us -> 443 us  [the longest x48 171 us: dot_cols(): lax.dot_general(left, right, (((1,), (1,)), ((), ())), preferred_element_...]
    ppermute x110 -> x0, waiting for transfers between devices: 320 us -> none  [the longest x55 320 us: fwd_tick(): return (lax.ppermute(layer_out, 'stage', fwd_perm), layer_in)]
    dynamic_slice x331 -> x1, local copies, waits for them, and re-layouts: 228 us -> 2.38 us  [body(): lax.dynamic_slice_in_dim(cot_out, stage * own, own, 0).reshape(-1, width)]
    all_gather x3 -> x7, waiting for transfers between devices: 88.5 us -> 273 us  [the longest x6 273 us: whole(): full = lax.all_gather(w[v, 0], GRP, axis=0, tiled=True)]
    reduce_sum x110 -> x1, other arithmetic: 121 us -> 1.42 us  [block_forward(): r = lax.rsqrt(jnp.mean(h * h, axis=-1, keepdims=True) + NORM_EPS)]
    dynamic_update_slice x55 -> x0, other arithmetic: 104 us -> none  [body(): last_fwd, seen_in = lax.scan(fwd_tick, zero_rows, tick_ids)]
    psum x1 -> x0, waiting for transfers between devices: 99.3 us -> none  [body(): lax.psum(first_grad, 'stage').reshape(n_micro, rows_dev, seq_len, dmodel)]
  transfers between devices with their start and end apart: 117 -> 13, of which waited for: 62 -> 11; matrix products, arithmetic and copies ran while one was open for 19% -> 12% of each run, Pallas kernels for 0% -> 0%
where the time goes in v1:
time: 1860 us; the launch traced here: 1850 us
  waiting for transfers between devices  1300 us (70%)
  matrix products  443 us (24%)
  local copies, waits for them, and re-layouts  62.5 us (3%)
  other arithmetic  24.2 us (1%)
    reduce_scatter x6, waiting for transfers between devices, body(): lax.psum_scatter(stacked, GRP, scatter_dimension=0, tiled=True)  1030 us
    all_gather x6, waiting for transfers between devices, whole(): full = lax.all_gather(w[v, 0], GRP, axis=0, tiled=True)  273 us
    dot_general x48, matrix products, dot_cols(): lax.dot_general(left, right, (((1,), (1,)), ((), ())), preferred_element_...  171 us
    dot_general x47, matrix products, dot_f32(): return jnp.dot(left, right, preferred_element_type=jnp.float32)  162 us
    dot_general x48, matrix products, dot_rows(): lax.dot_general(left, right, (((0,), (0,)), ((), ())), preferred_element_...  110 us
    unnamed x489, local copies, waits for them, and re-layouts  55 us
  transfers between devices with their start and end apart: 13, of which 11 were waited for; matrix products, arithmetic and copies ran while one was open for 12% of the time, Pallas kernels for 0%

profile of v1, /device:TPU:0, one launch (start us, length us, event | category | flops | bytes accessed | tf_op | source)
XLA Modules:
  0.0 1849.5 jit_solution(15971952948178222135)
XLA Ops:
  20.9 55.5 %all-gather.16.cloned.1.call-done = bf16[1,1,2048,1024]{3,2,1,0:T(8,128)(2,1)} async-done(((bf16[1,1,64,1024]{3,2,1,0:T(8,128)(2,1)}), bf16[1,1,2048,1024]{3,2,1,0:T(8,128)(2,1)}) %all-gather.16.cloned.1.call-update) | async-done | bytes 4194320 | tf_op jit(solution)/shard_map/all_gather | solution.py:67
  76.4 4.7 fusion.52
  81.2 58.8 %all-gather.18.cloned.1.call-done = bf16[1,1,2048,1024]{3,2,1,0:T(8,128)(2,1)} async-done(((bf16[1,1,64,1024]{3,2,1,0:T(8,128)(2,1)}), bf16[1,1,2048,1024]{3,2,1,0:T(8,128)(2,1)}) %all-gather.18.cloned.1.call-update) | async-done | bytes 4194320 | tf_op jit(solution)/shard_map/all_gather | solution.py:67
  140.0 6.4 multiply_convert_fusion.47
  146.4 57.1 %all-gather.20.cloned.1.call-done = bf16[1,1,8192,256]{3,2,1,0:T(8,128)(2,1)} async-done(((bf16[1,1,256,256]{3,2,1,0:T(8,128)(2,1)}), bf16[1,1,8192,256]{3,2,1,0:T(8,128)(2,1)}) %all-gather.20.cloned.1.call-update) | async-done | bytes 4194320 | tf_op jit(solution)/shard_map/all_gather | solution.py:67
  209.9 4.9 multiply_convert_fusion.46
  220.1 4.9 multiply_convert_fusion.45
  230.8 5.2 multiply_convert_fusion.44
  241.3 5.0 multiply_convert_fusion.43
  252.1 5.0 multiply_convert_fusion.42
  262.4 5.1 multiply_convert_fusion.41
  273.2 5.3 multiply_convert_fusion.40
  282.0 4.9 fusion.84
  286.9 44.6 %all-gather.24.cloned.1.call-done = bf16[1,1,2048,1024]{3,2,1,0:T(8,128)(2,1)} async-done(((bf16[1,1,64,1024]{3,2,1,0:T(8,128)(2,1)}), bf16[1,1,2048,1024]{3,2,1,0:T(8,128)(2,1)}) %all-gather.24.cloned.1.call-update) | async-done | bytes 4194320 | tf_op jit(solution)/shard_map/all_gather | solution.py:67
  331.5 6.6 multiply_convert_fusion.39
  338.1 56.8 %all-gather.26.cloned.1.call-done = bf16[1,1,8192,256]{3,2,1,0:T(8,128)(2,1)} async-done(((bf16[1,1,256,256]{3,2,1,0:T(8,128)(2,1)}), bf16[1,1,8192,256]{3,2,1,0:T(8,128)(2,1)}) %all-gather.26.cloned.1.call-update) | async-done | bytes 4194320 | tf_op jit(solution)/shard_map/all_gather | solution.py:67
  401.3 4.9 multiply_convert_fusion.38
  411.4 5.1 multiply_convert_fusion.37
  421.8 4.7 multiply_convert_fusion.36
  431.6 5.0 multiply_convert_fusion.35
  441.8 4.9 multiply_convert_fusion.34
  451.8 5.2 multiply_convert_fusion.33
  464.8 6.3 multiply_convert_fusion.31
  477.5 7.1 multiply_convert_fusion.29
  491.7 6.5 multiply_convert_fusion.27
  505.7 6.5 multiply_convert_fusion.25
  520.1 6.8 multiply_convert_fusion.23
  533.8 6.5 multiply_convert_fusion.21
  547.4 5.5 multiply_convert_fusion.19
  558.6 6.4 multiply_convert_fusion.17
  573.7 5.4 multiply_convert_fusion.15
  586.1 5.7 multiply_convert_fusion.13
  597.5 5.3 multiply_convert_fusion.11
  608.4 5.5 multiply_convert_fusion.9
  618.5 6.5 multiply_convert_fusion.7
  632.0 6.4 multiply_convert_fusion.5
  645.5 6.6 multiply_convert_fusion.3
  659.2 6.3 multiply_convert_fusion.1
  675.0 4.3 convolution_dynamic-update-slice_fusion.14
  719.0 4.3 convolution_dynamic-update-slice_fusion.30
  739.7 4.3 convolution_dynamic-update-slice_fusion.22
  804.3 101.9 %reduce-scatter.15.cloned.1.call-done = f32[256,256]{1,0:T(8,128)} async-done(((f32[8192,256]{1,0:T(8,128)}), f32[256,256]{1,0:T(8,128)}) %reduce-scatter.15.cloned.1.call-update) | async-done | bytes 262160 | tf_op jit(solution)/shard_map/reduce_scatter | solution.py:84
  906.2 185.7 %reduce-scatter.17.cloned.1.call-done = f32[256,256]{1,0:T(8,128)} async-done(((f32[8192,256]{1,0:T(8,128)}), f32[256,256]{1,0:T(8,128)}) %reduce-scatter.17.cloned.1.call-update) | async-done | bytes 262160 | tf_op jit(solution)/shard_map/reduce_scatter | solution.py:84
  1093.8 183.7 %reduce-scatter.11.cloned.1.call-done = f32[64,1024]{1,0:T(8,128)} async-done(((f32[2048,1024]{1,0:T(8,128)}), f32[64,1024]{1,0:T(8,128)}) %reduce-scatter.11.cloned.1.call-update) | async-done | bytes 262160 | tf_op jit(solution)/shard_map/reduce_scatter | solution.py:84
  1277.5 185.7 %reduce-scatter.13.cloned.1.call-done = f32[64,1024]{1,0:T(8,128)} async-done(((f32[2048,1024]{1,0:T(8,128)}), f32[64,1024]{1,0:T(8,128)}) %reduce-scatter.13.cloned.1.call-update) | async-done | bytes 262160 | tf_op jit(solution)/shard_map/reduce_scatter | solution.py:84
  1465.1 183.7 %reduce-scatter.7.cloned.1.call-done = f32[64,1024]{1,0:T(8,128)} async-done(((f32[2048,1024]{1,0:T(8,128)}), f32[64,1024]{1,0:T(8,128)}) %reduce-scatter.7.cloned.1.call-update) | async-done | bytes 262160 | tf_op jit(solution)/shard_map/reduce_scatter | solution.py:84
  1648.8 185.7 %reduce-scatter.9.cloned.1.call-done = f32[64,1024]{1,0:T(8,128)} async-done(((f32[2048,1024]{1,0:T(8,128)}), f32[64,1024]{1,0:T(8,128)}) %reduce-scatter.9.cloned.1.call-update) | async-done | bytes 262160 | tf_op jit(solution)/shard_map/reduce_scatter | solution.py:84
  1836.4 6.1 copy.61
  (713 shorter events, 327.1 us)
Async XLA Ops:
  7.2 69.3 %all-gather.16.cloned.1.call-start = ((), (), s32[]{:S(2)}) async-start(), calls=%async_computation.13 | async-start | bytes 4325376 | tf_op jit(solution)/shard_map/all_gather | solution.py:67
  8.9 131.1 %all-gather.18.cloned.1.call-start = ((), (), s32[]{:S(2)}) async-start(), calls=%async_computation.14 | async-start | bytes 4325376 | tf_op jit(solution)/shard_map/all_gather | solution.py:67
  10.7 192.9 %all-gather.20.cloned.1.call-start = ((), (), s32[]{:S(2)}) async-start(), calls=%async_computation.15 | async-start | bytes 4325376 | tf_op jit(solution)/shard_map/all_gather | solution.py:67
  12.4 269.6 %all-gather.22.cloned.1.call-start = ((), (), s32[]{:S(2)}) async-start(), calls=%async_computation.16 | async-start | bytes 4325376 | tf_op jit(solution)/shard_map/all_gather | solution.py:67
  13.0 318.5 %all-gather.24.cloned.1.call-start = ((), (), s32[]{:S(2)}) async-start(), calls=%async_computation.17 | async-start | bytes 4325376 | tf_op jit(solution)/shard_map/all_gather | solution.py:67
  13.6 381.3 %all-gather.26.cloned.1.call-start = ((), (), s32[]{:S(2)}) async-start(), calls=%async_computation.18 | async-start | bytes 4325376 | tf_op jit(solution)/shard_map/all_gather | solution.py:67
  14.2 790.1 %all-gather.14.cloned.1.call-start = ((), (), s32[]{:S(2)}) async-start(), calls=%async_computation.6 | async-start | bytes 7077888 | tf_op jit(solution)/shard_map/all_gather | solution.py:85
  17.1 64.1 %copy-start.191 = (f32[1536]{0:T(1024)}, f32[1536]{0:T(1024)S(1)}, u32[]{:S(2)}) copy-start(f32[1536]{0:T(1024)S(1)} %rsqrt.147) | copy-start | bytes 18436
  18.5 121.5 %copy-start.91 = (bf16[1536,256]{1,0:T(8,128)(2,1)}, bf16[1536,256]{1,0:T(8,128)(2,1)S(1)}, u32[]{:S(2)}) copy-start(bf16[1536,256]{1,0:T(8,128)(2,1)S(1)} %fusion.48) | copy-start | bytes 2359300
  206.6 8.2 copy-start
  217.3 7.7 copy-start.2
  227.5 8.5 copy-start.4
  238.5 7.8 copy-start.6
  248.8 8.3 copy-start.8
  259.6 7.8 copy-start.10
  269.9 8.6 copy-start.12
  273.2 5.3 copy-start.28
  281.0 113.9 %copy-start.14 = (f32[1536,256]{1,0:T(8,128)}, f32[1536,256]{1,0:T(8,128)S(1)}, u32[]{:S(2)}) copy-start(f32[1536,256]{1,0:T(8,128)S(1)} %get-tuple-element.85) | copy-start | bytes 4718596
  282.0 49.5 %copy-start.111 = (bf16[1536,256]{1,0:T(8,128)(2,1)}, bf16[1536,256]{1,0:T(8,128)(2,1)S(1)}, u32[]{:S(2)}) copy-start(bf16[1536,256]{1,0:T(8,128)(2,1)S(1)} %multiply_convert_fusion.58) | copy-start | bytes 2359300
  398.0 8.2 copy-start.16
  408.7 7.9 copy-start.18
  464.7 6.5 copy-start.23
  477.4 12.9 copy-start.138
  490.8 7.4 copy-start.140
  504.2 13.4 copy-start.143
  518.1 14.1 copy-start.145
  520.1 6.8 copy-start.136
  532.7 13.0 copy-start.147
  546.3 11.1 copy-start.149
  557.9 12.5 copy-start.151
  570.9 14.4 copy-start.152
  573.7 5.5 copy-start.133
  585.8 10.4 copy-start.154
  596.8 10.5 copy-start.156
  607.7 10.0 copy-start.158
  618.2 12.3 copy-start.160
  631.0 12.9 copy-start.162
  644.4 13.1 copy-start.164
  658.1 13.9 copy-start.168
  674.6 231.7 %reduce-scatter.15.cloned.1.call-start = ((), (), s32[]{:S(2)}) async-start(), calls=%async_computation.11 | async-start | bytes 8650752 | tf_op jit(solution)/shard_map/reduce_scatter | solution.py:84
  696.0 396.0 %reduce-scatter.17.cloned.1.call-start = ((), (), s32[]{:S(2)}) async-start(), calls=%async_computation.12 | async-start | bytes 8650752 | tf_op jit(solution)/shard_map/reduce_scatter | solution.py:84
  707.7 6.1 slice-start.8
  709.8 5.3 slice-start.9
  718.7 558.8 %reduce-scatter.11.cloned.1.call-start = ((), (), s32[]{:S(2)}) async-start(), calls=%async_computation.9 | async-start | bytes 8650752 | tf_op jit(solution)/shard_map/reduce_scatter | solution.py:84
  739.6 723.6 %reduce-scatter.13.cloned.1.call-start = ((), (), s32[]{:S(2)}) async-start(), calls=%async_computation.10 | async-start | bytes 8650752 | tf_op jit(solution)/shard_map/reduce_scatter | solution.py:84
  760.7 5.2 copy-start.95
  760.7 888.1 %reduce-scatter.7.cloned.1.call-start = ((), (), s32[]{:S(2)}) async-start(), calls=%async_computation.7 | async-start | bytes 8650752 | tf_op jit(solution)/shard_map/reduce_scatter | solution.py:84
  783.1 1051.4 %reduce-scatter.9.cloned.1.call-start = ((), (), s32[]{:S(2)}) async-start(), calls=%async_computation.8 | async-start | bytes 8650752 | tf_op jit(solution)/shard_map/reduce_scatter | solution.py:84
  (209 other events, 601.6 us)
Sparse Core Ops, SparseCore 0:
  11.5 64.8 all-gather.15
  79.4 60.5 all-gather.17
  143.0 60.5 all-gather.19
  207.0 60.5 all-gather.21
  270.9 60.5 all-gather.23
  334.3 60.5 all-gather.25
  674.7 43.5 all-gather.13
  720.5 185.6 reduce-scatter.14
  908.5 183.3 reduce-scatter.16
  1094.1 183.3 reduce-scatter.10
  1279.8 183.3 reduce-scatter.12
  1465.4 183.3 reduce-scatter.6
  1651.1 183.3 reduce-scatter.8

commit v2 on v1

v2 whole, which is shorter than its diff:
```python
import functools

import jax
import jax.numpy as jnp
from jax import lax
from jax.experimental import pallas as pl
from jax.experimental.pallas import tpu as pltpu
from jax.sharding import PartitionSpec as P

NORM_EPS = 1e-6
MESH = pl.DeviceIdType.MESH
SLOTS = 8
FWD_LEAD = 7
BWD_DRAIN = 8
LANE, WIDE, HALF = 128, 256, 512
PIECE, SUB = 64, 32
F32 = jnp.float32
BF16 = jnp.bfloat16


class Place:
    def __init__(self):
        self.z, self.s = lax.axis_index("data"), lax.axis_index("stage")
        self.core, self.x, self.y = self.s % 2, (self.s // 2) % 2, self.s // 4
        self.zn, self.zf = self.z % 2, self.z // 2
        self.to_x = (self.z, self.s + 2 - 4 * self.x)
        self.to_y = (self.z, self.s + 4 - 8 * self.y)
        self.to_core = (self.z, self.s + 1 - 2 * self.core)
        self.to_zn = (self.z + 1 - 2 * self.zn, self.s)
        self.to_zf = (self.z + 2 - 4 * self.zf, self.s)


def col(start, size):
    return pl.ds(pl.multiple_of(start, LANE), size)


def narrow(core, hi, lo):
    return HALF * core + WIDE * hi + LANE * lo


def remote(src, dst, ssem, rsem, to):
    return pltpu.make_async_remote_copy(src_ref=src, dst_ref=dst, send_sem=ssem, recv_sem=rsem, device_id=to, device_id_type=MESH)


def wait_bytes(ref, sem):
    pltpu.make_async_copy(ref, ref, sem).wait()


def enter(here, n_stage):
    barrier = pltpu.get_barrier_semaphore()
    peers = [(here.z, (here.s + k) % n_stage) for k in range(1, n_stage)] + [here.to_zn, here.to_zf]
    for peer in peers:
        pl.semaphore_signal(barrier, inc=1, device_id=peer, device_id_type=MESH)
    pl.semaphore_wait(barrier, len(peers))


def mat_rows(left, right):
    return lax.dot_general(left, right, (((0,), (0,)), ((), ())), preferred_element_type=F32)


def mat_cols(left, right):
    return lax.dot_general(left, right, (((1,), (1,)), ((), ())), preferred_element_type=F32)


def mat(left, right):
    return jnp.dot(left, right, preferred_element_type=F32)


def square(w_ref, at, m, k):
    return w_ref[at, m, :, :, :, WIDE * k : WIDE * k + WIDE].reshape(WIDE, WIDE)


def out_square(w_ref, at, k):
    return jnp.concatenate([w_ref[at, 2, k // 2, k % 2, :, WIDE * j : WIDE * j + WIDE] for j in range(4)], axis=0)


def fwd_kernel(n_stage, act, wg, wi, wo, w_all, h_all, w, h, s0, r0, ssem, rsem, lsem, hsem, wsem):
    here = Place()
    z, s, zn, zf = here.z, here.s, here.zn, here.zf
    n_block = w.shape[0]
    n_v = n_block // n_stage
    rows = h.shape[1]
    tile = min(WIDE, rows // 2)
    c_g, c_i = narrow(here.core, here.x, here.y), narrow(here.core, here.y, here.x)
    c_x, c_y, c_c = narrow(here.core, here.x, 0), narrow(here.core, here.y, 0), narrow(here.core, 0, 0)

    enter(here, n_stage)
    load = pltpu.make_async_copy(act.at[s], h.at[0], lsem)
    load.start()

    def scatter(v, k):
        q = (s + k) % n_stage
        core, x, y = q % 2, (q // 2) % 2, q // 4
        d_g, d_i = narrow(core, x, y), narrow(core, y, x)
        c = v * n_stage + s
        moves = (
            (wg.at[v, 0, :, col(d_g, LANE)], w.at[c, 0, zf, zn, :, col(d_g, LANE)]),
            (wi.at[v, 0, :, col(d_i, LANE)], w.at[c, 1, zf, zn, :, col(d_i, LANE)]),
            (wo.at[v, 0, pl.ds(pl.multiple_of(PIECE * (2 * core + x), SUB), SUB), col(LANE * y, LANE)], w.at[c, 2, zf, zn, 0:SUB, col(d_g, LANE)]),
            (wo.at[v, 0, pl.ds(pl.multiple_of(PIECE * (2 * core + y) + SUB, SUB), SUB), col(LANE * x, LANE)], w.at[c, 2, zf, zn, SUB:PIECE, col(d_i, LANE)]),
        )
        for src, dst in moves:
            if k == 0:
                pltpu.make_async_copy(src, dst, r0.at[c]).start()
            else:
                remote(src, dst, s0.at[v], r0.at[c], (z, q)).start()

    for v in range(n_v):
        for k in range(n_stage):
            scatter(v, k)

    def parts(phase, c):
        if phase == 1:
            return (
                (w.at[c, 0, zf, zn, :, col(c_g, LANE)], here.to_zf),
                (w.at[c, 1, zf, zn, :, col(c_i, LANE)], here.to_zf),
                (w.at[c, 2, zf, zn, 0:SUB, col(c_g, LANE)], here.to_zf),
                (w.at[c, 2, zf, zn, SUB:PIECE, col(c_i, LANE)], here.to_zf),
            )
        if phase == 2:
            return (
                (w.at[c, 0, :, zn, :, col(c_g, LANE)], here.to_zn),
                (w.at[c, 1, :, zn, :, col(c_i, LANE)], here.to_zn),
                (w.at[c, 2, :, zn, 0:SUB, col(c_g, LANE)], here.to_y),
                (w.at[c, 2, :, zn, SUB:PIECE, col(c_i, LANE)], here.to_x),
            )
        if phase == 3:
            return (
                (w.at[c, 0, :, :, :, col(c_g, LANE)], here.to_y),
                (w.at[c, 1, :, :, :, col(c_i, LANE)], here.to_x),
                (w.at[c, 2, :, zn, 0:SUB, col(c_x, WIDE)], here.to_x),
                (w.at[c, 2, :, zn, SUB:PIECE, col(c_y, WIDE)], here.to_y),
            )
        if phase == 4:
            return (
                (w.at[c, 0, :, :, :, col(c_x, WIDE)], here.to_x),
                (w.at[c, 1, :, :, :, col(c_y, WIDE)], here.to_y),
                (w.at[c, 2, :, zn, :, col(c_c, HALF)], here.to_zn),
            )
        return ((w.at[c, :, :, :, :, col(c_c, HALF)], here.to_core),)

    def total(phase, c):
        if phase == 1:
            return w.at[c, :, 0, 0, :, 0:LANE]
        if phase == 2:
            return w.at[c, :, :, 0, :, 0:LANE]
        return w.at[c, :, :, :, :, 0 : {3: LANE, 4: WIDE, 5: HALF}[phase]]

    def arrived(phase, c):
        if phase == 0:
            wait_bytes(total(1, c), r0.at[c])
        else:
            slot = c % SLOTS
            wait_bytes(total(phase, c), rsem.at[phase - 1, slot])
            wait_bytes(total(phase, c), ssem.at[phase - 1, slot])

    def advance(phase, c):
        @pl.when((c >= 0) & (c < n_block))
        def _():
            arrived(phase - 1, c)
            slot = c % SLOTS
            for ref, to in parts(phase, c):
                remote(ref, ref, ssem.at[phase - 1, slot], rsem.at[phase - 1, slot], to).start()

    def one_tile(c, i):
        at = pl.ds(pl.multiple_of(i * tile, tile), tile)
        x32 = h[c, at, :].astype(F32)
        inv = lax.rsqrt(jnp.mean(x32 * x32, axis=-1, keepdims=True) + NORM_EPS)
        n = (x32 * inv).astype(BF16)
        acc = x32
        for k in range(4):
            a = mat(n, square(w, c, 0, k))
            b = mat(n, square(w, c, 1, k))
            u = (a * jax.nn.sigmoid(a) * b).astype(BF16)
            acc += mat(u, out_square(w, c, k))
        h[c + 1, at, :] = acc.astype(BF16)

    per_half = rows // tile // 2

    def half_step(i, carry):
        c = i // 2 - FWD_LEAD
        second = i % 2 == 1

        @pl.when(i % 2 == 0)
        def _():
            advance(4, c + 2)
            advance(2, c + 5)

            @pl.when(c == 0)
            def _():
                load.wait()

            @pl.when(c >= 0)
            def _():
                arrived(5, c)

        @pl.when(second)
        def _():
            advance(5, c + 1)
            advance(3, c + 4)
            advance(1, c + 7)

            @pl.when(c >= 0)
            def _():
                pltpu.make_async_copy(w.at[c], w_all.at[c], wsem.at[c]).start()
                pltpu.make_async_copy(h.at[c], h_all.at[c], hsem.at[c]).start()

        @pl.when((c >= 0) & (c < n_block - 1))
        def _():
            def body(j, carry):
                one_tile(c, (i % 2) * per_half + j)
                return carry

            lax.fori_loop(0, per_half, body, 0)

        return carry

    lax.fori_loop(0, 2 * (n_block + FWD_LEAD), half_step, 0)
    for v in range(n_v):
        wait_bytes(w.at[0, :, 0, 0, :, 0 : LANE * (n_stage - 1)], s0.at[v])

    def drain(c, carry):
        pltpu.make_async_copy(w.at[c], w_all.at[c], wsem.at[c]).wait()
        pltpu.make_async_copy(h.at[c], h_all.at[c], hsem.at[c]).wait()
        return carry

    lax.fori_loop(0, n_block, drain, 0)


def bwd_kernel(n_stage, cot, w_all, h_all, gg, gi, go, ga, w, h, e, g, x1, x2g, x2i, x2o, x3g, x3i, x3a, x3b, x4g, x4i, x4a, x4b, x5g, x5i, x5a, x5b, fg, fi, fa, fb, ssem, rsem, own, fsem, wsem, hsem, esem, a1s, a1r, a2s, a2r, a3s, a3r):
    here = Place()
    z, s, zn, zf, x, y, core = here.z, here.s, here.zn, here.zf, here.x, here.y, here.core
    n_block = w_all.shape[0]
    n_v = n_block // n_stage
    rows = h.shape[1]
    tile = min(WIDE, rows // 2)
    c_g, c_i = narrow(core, x, y), narrow(core, y, x)

    load_e = pltpu.make_async_copy(cot.at[s], e.at[s], esem)
    load_e.start()

    def fetch(b):
        c, slot = n_block - 1 - b, b % 2
        return (
            pltpu.make_async_copy(w_all.at[c], w.at[slot], wsem.at[slot]),
            pltpu.make_async_copy(h_all.at[c], h.at[slot], hsem.at[slot]),
        )

    for copy in fetch(0):
        copy.start()
    enter(here, n_stage)
    load_e.wait()

    def total(phase, slot):
        if phase == 1:
            return x1.at[slot]
        if phase == 2:
            return x1.at[slot, :, :, :, :, 0:WIDE]
        if phase == 3:
            return x1.at[slot, :, :, :, :, 0:LANE]
        if phase == 4:
            return x1.at[slot, :, :, 0, :, 0:LANE]
        return x1.at[slot, :, 0, 0, :, 0:LANE]

    def push(phase, b, moves):
        slot = b % SLOTS
        for src, dst, to in moves:
            remote(src, dst, ssem.at[phase - 1, slot], rsem.at[phase - 1, slot], to).start()

    def taken(phase, b):
        slot = b % SLOTS
        wait_bytes(total(phase, slot), rsem.at[phase - 1, slot])
        wait_bytes(total(phase, slot), ssem.at[phase - 1, slot])

    def when_valid(b, fn):
        @pl.when((b >= 0) & (b < n_block))
        def _():
            fn(b)

    def q1(b):
        push(1, b, ((g.at[b % 2, :, :, :, :, col(HALF - HALF * core, HALF)], x1.at[b % SLOTS], here.to_core),))

    def q2(b):
        taken(1, b)
        q, p = b % SLOTS, b % 2
        for m in range(3):
            for f in range(2):
                for k in range(2):
                    x1[q, m, f, k] += g[p, m, f, k, :, col(HALF * core, HALF)]
        push(2, b, (
            (x1.at[q, 0, :, :, :, col(WIDE - WIDE * x, WIDE)], x2g.at[q], here.to_x),
            (x1.at[q, 1, :, :, :, col(WIDE - WIDE * y, WIDE)], x2i.at[q], here.to_y),
            (x1.at[q, 2, :, 1 - zn], x2o.at[q], here.to_zn),
        ))

    def q3(b):
        taken(2, b)
        q = b % SLOTS
        for f in range(2):
            for k in range(2):
                x2g[q, f, k] += x1[q, 0, f, k, :, col(WIDE * x, WIDE)]
                x2i[q, f, k] += x1[q, 1, f, k, :, col(WIDE * y, WIDE)]
            x2o[q, f] += x1[q, 2, f, zn]
        push(3, b, (
            (x2g.at[q, :, :, :, col(LANE - LANE * y, LANE)], x3g.at[q], here.to_y),
            (x2i.at[q, :, :, :, col(LANE - LANE * x, LANE)], x3i.at[q], here.to_x),
            (x2o.at[q, :, 0:SUB, col(WIDE - WIDE * x, WIDE)], x3a.at[q], here.to_x),
            (x2o.at[q, :, SUB:PIECE, col(WIDE - WIDE * y, WIDE)], x3b.at[q], here.to_y),
        ))

    def q4(b):
        taken(3, b)
        q = b % SLOTS
        for f in range(2):
            for k in range(2):
                x3g[q, f, k] += x2g[q, f, k, :, col(LANE * y, LANE)]
                x3i[q, f, k] += x2i[q, f, k, :, col(LANE * x, LANE)]
            x3a[q, f] += x2o[q, f, 0:SUB, col(WIDE * x, WIDE)]
            x3b[q, f] += x2o[q, f, SUB:PIECE, col(WIDE * y, WIDE)]
        push(4, b, (
            (x3g.at[q, :, 1 - zn], x4g.at[q], here.to_zn),
            (x3i.at[q, :, 1 - zn], x4i.at[q], here.to_zn),
            (x3a.at[q, :, :, col(LANE - LANE * y, LANE)], x4a.at[q], here.to_y),
            (x3b.at[q, :, :, col(LANE - LANE * x, LANE)], x4b.at[q], here.to_x),
        ))

    def q5(b):
        taken(4, b)
        q = b % SLOTS
        for f in range(2):
            x4g[q, f] += x3g[q, f, zn]
            x4i[q, f] += x3i[q, f, zn]
            x4a[q, f] += x3a[q, f, :, col(LANE * y, LANE)]
            x4b[q, f] += x3b[q, f, :, col(LANE * x, LANE)]
        push(5, b, (
            (x4g.at[q, 1 - zf], x5g.at[q], here.to_zf),
            (x4i.at[q, 1 - zf], x5i.at[q], here.to_zf),
            (x4a.at[q, 1 - zf], x5a.at[q], here.to_zf),
            (x4b.at[q, 1 - zf], x5b.at[q], here.to_zf),
        ))

    def q6(b):
        taken(5, b)
        q = b % SLOTS
        c = n_block - 1 - b
        v, p = c // n_stage, c % n_stage
        fg[b] = x5g[q] + x4g[q, zf]
        fi[b] = x5i[q] + x4i[q, zf]
        fa[b] = x5a[q] + x4a[q, zf]
        fb[b] = x5b[q] + x4b[q, zf]
        moves = (
            (fg.at[b], gg.at[v, 0, :, col(c_g, LANE)]),
            (fi.at[b], gi.at[v, 0, :, col(c_i, LANE)]),
            (fa.at[b], go.at[v, 0, pl.ds(pl.multiple_of(PIECE * (2 * core + x), SUB), SUB), col(LANE * y, LANE)]),
            (fb.at[b], go.at[v, 0, pl.ds(pl.multiple_of(PIECE * (2 * core + y) + SUB, SUB), SUB), col(LANE * x, LANE)]),
        )

        @pl.when(p == s)
        def _():
            for src, dst in moves:
                pltpu.make_async_copy(src, dst, own.at[b]).start()

        @pl.when(p != s)
        def _():
            for src, dst in moves:
                remote(src, dst, own.at[b], fsem.at[v], (z, p)).start()

    def one_tile(b, i):
        at = pl.ds(pl.multiple_of(i * tile, tile), tile)
        p = b % 2
        first = i == 0
        x32 = h[p, at, :].astype(F32)
        inv = lax.rsqrt(jnp.mean(x32 * x32, axis=-1, keepdims=True) + NORM_EPS)
        hr = x32 * inv
        n = hr.astype(BF16)
        et = e[s, at, :]
        q = jnp.zeros((tile, WIDE), F32)

        def add(m, k, value):
            for f in range(2):
                for r in range(2):
                    part = value[LANE * f + PIECE * r : LANE * f + PIECE * r + PIECE]
                    old = g[p, m, f, r, :, WIDE * k : WIDE * k + WIDE]
                    g[p, m, f, r, :, WIDE * k : WIDE * k + WIDE] = part + jnp.where(first, 0.0, old)

        for k in range(4):
            wg, wi, wo = square(w, p, 0, k), square(w, p, 1, k), out_square(w, p, k)
            a = mat(n, wg)
            bb = mat(n, wi)
            t = mat_cols(et, wo)
            sg = jax.nn.sigmoid(a)
            act = a * sg
            u = (act * bb).astype(BF16)
            da = (t * bb * sg * (1.0 + a * (1.0 - sg))).astype(BF16)
            db = (t * act).astype(BF16)
            q += mat_cols(da, wg) + mat_cols(db, wi)
            add(0, k, mat_rows(n, da))
            add(1, k, mat_rows(n, db))
            do = mat_rows(u, et)
            for j in range(4):
                old = g[p, 2, k // 2, k % 2, :, WIDE * j : WIDE * j + WIDE]
                g[p, 2, k // 2, k % 2, :, WIDE * j : WIDE * j + WIDE] = do[PIECE * j : PIECE * j + PIECE] + jnp.where(first, 0.0, old)
        grad = et.astype(F32) + inv * (q - hr * jnp.mean(q * hr, axis=-1, keepdims=True))
        e[s, at, :] = grad.astype(BF16)

    per_half = rows // tile // 2

    def half_step(i, carry):
        b = i // 2

        @pl.when(i % 2 == 0)
        def _():
            when_valid(b - 8, q6)
            when_valid(b - 5, q4)
            when_valid(b - 2, q2)

            @pl.when(b < n_block)
            def _():
                for copy in fetch(b):
                    copy.wait()

            @pl.when(b + 1 < n_block)
            def _():
                for copy in fetch(b + 1):
                    copy.start()

        @pl.when(i % 2 == 1)
        def _():
            when_valid(b - 6, q5)
            when_valid(b - 3, q3)

        @pl.when(b < n_block)
        def _():
            def body(j, carry):
                one_tile(b, (i % 2) * per_half + j)
                return carry

            lax.fori_loop(0, per_half, body, 0)

            @pl.when(i % 2 == 1)
            def _():
                q1(b)

        return carry

    lax.fori_loop(0, 2 * n_block, half_step, 0)

    half = rows // 2
    lo, hi = pl.ds(0, half), pl.ds(half, half)
    sx, sy = here.to_x[1], here.to_y[1]
    first = [remote(e.at[s, lo], e.at[s, lo], a1s.at[0], a1r.at[0], here.to_x), remote(e.at[s, hi], e.at[s, hi], a1s.at[1], a1r.at[1], here.to_y)]
    for copy in first:
        copy.start()
    lax.fori_loop(2 * n_block, 2 * n_block + 4, half_step, 0)
    for copy in first:
        copy.wait()
    second = [
        remote(e.at[s, lo], e.at[s, lo], a2s.at[0], a2r.at[0], here.to_y),
        remote(e.at[sx, lo], e.at[sx, lo], a2s.at[1], a2r.at[1], here.to_y),
        remote(e.at[s, hi], e.at[s, hi], a2s.at[2], a2r.at[2], here.to_x),
        remote(e.at[sy, hi], e.at[sy, hi], a2s.at[3], a2r.at[3], here.to_x),
    ]
    for copy in second:
        copy.start()
    lax.fori_loop(2 * n_block + 4, 2 * (n_block + BWD_DRAIN) + 1, half_step, 0)
    for copy in second:
        copy.wait()
    last = []
    for k in range(n_stage // 2):
        q = 2 * k + core
        last.append(remote(e.at[q], ga.at[q], a3s.at[k], a3r.at[k], here.to_core))
        last.append(pltpu.make_async_copy(e.at[q], ga.at[q], a3s.at[n_stage // 2 + k]))
    for copy in last:
        copy.start()

    def finish(b, carry):
        wait_bytes(total(5, 0), own.at[b])
        return carry

    lax.fori_loop(0, n_block, finish, 0)
    for v in range(n_v):
        wait_bytes(g.at[0, :, 0, 0, :, 0 : LANE * (n_stage - 1)], fsem.at[v])
    for copy in last:
        copy.wait()


def solution(mesh):
    n_stage = mesh.shape["stage"]
    act_spec = P(None, "data", None, None)
    w_spec = P(None, "stage", "data", None)
    hbm = pl.BlockSpec(memory_space=pltpu.HBM)
    dma = pltpu.SemaphoreType.DMA

    def body(act_in, cot_out, w_gate, w_in, w_out):
        n_micro, n_seq, n_tok, width = act_in.shape
        n_v, _, _, ffn = w_gate.shape
        n_block = n_v * n_stage
        rows = n_micro // n_stage * n_seq * n_tok
        act = act_in.reshape(n_stage, rows, width)
        cot = cot_out.reshape(n_stage, rows, width)
        block = (3, 2, 2, PIECE, ffn)
        flops = 2 * rows * width * ffn * n_block

        def f32(*shape):
            return pltpu.VMEM(shape, F32)

        w_all, h_all = pl.pallas_call(
            functools.partial(fwd_kernel, n_stage),
            name="forward",
            out_shape=(jax.ShapeDtypeStruct((n_block, *block), BF16), jax.ShapeDtypeStruct((n_block, rows, width), BF16)),
            in_specs=[hbm] * 4,
            out_specs=[hbm] * 2,
            scratch_shapes=[
                pltpu.VMEM((n_block, *block), BF16),
                pltpu.VMEM((n_block, rows, width), BF16),
                dma((n_v,)),
                dma((n_block,)),
                dma((5, SLOTS)),
                dma((5, SLOTS)),
                dma,
                dma((n_block,)),
                dma((n_block,)),
            ],
            compiler_params=pltpu.CompilerParams(collective_id=0, has_side_effects=True, vmem_limit_bytes=63 * 2**20),
            cost_estimate=pl.CostEstimate(flops=3 * flops, bytes_accessed=2**26, transcendentals=0),
        )(act, w_gate, w_in, w_out)
        n = SLOTS
        gg, gi, go, ga = pl.pallas_call(
            functools.partial(bwd_kernel, n_stage),
            name="backward",
            out_shape=(
                jax.ShapeDtypeStruct(w_gate.shape, F32),
                jax.ShapeDtypeStruct(w_in.shape, F32),
                jax.ShapeDtypeStruct(w_out.shape, F32),
                jax.ShapeDtypeStruct((n_stage, rows, width), BF16),
            ),
            in_specs=[hbm] * 3,
            out_specs=[hbm] * 4,
            scratch_shapes=[
                pltpu.VMEM((2, *block), BF16),
                pltpu.VMEM((2, rows, width), BF16),
                pltpu.VMEM((n_stage, rows, width), BF16),
                f32(2, *block),
                f32(n, 3, 2, 2, PIECE, HALF),
                f32(n, 2, 2, PIECE, WIDE),
                f32(n, 2, 2, PIECE, WIDE),
                f32(n, 2, PIECE, HALF),
                f32(n, 2, 2, PIECE, LANE),
                f32(n, 2, 2, PIECE, LANE),
                f32(n, 2, SUB, WIDE),
                f32(n, 2, SUB, WIDE),
                f32(n, 2, PIECE, LANE),
                f32(n, 2, PIECE, LANE),
                f32(n, 2, SUB, LANE),
                f32(n, 2, SUB, LANE),
                f32(n, PIECE, LANE),
                f32(n, PIECE, LANE),
                f32(n, SUB, LANE),
                f32(n, SUB, LANE),
                f32(n_block, PIECE, LANE),
                f32(n_block, PIECE, LANE),
                f32(n_block, SUB, LANE),
                f32(n_block, SUB, LANE),
                dma((5, SLOTS)),
                dma((5, SLOTS)),
                dma((n_block,)),
                dma((n_v,)),
                dma((2,)),
                dma((2,)),
                dma,
                dma((2,)),
                dma((2,)),
                dma((4,)),
                dma((4,)),
                dma((n_stage,)),
                dma((n_stage // 2,)),
            ],
            compiler_params=pltpu.CompilerParams(collective_id=1, has_side_effects=True, vmem_limit_bytes=63 * 2**20),
            cost_estimate=pl.CostEstimate(flops=8 * flops, bytes_accessed=2**26, transcendentals=0),
        )(cot, w_all, h_all)
        return ga.reshape(act_in.shape), gg, gi, go

    return jax.shard_map(body, mesh=mesh, in_specs=(act_spec, act_spec, w_spec, w_spec, w_spec), out_specs=(act_spec, w_spec, w_spec, w_spec), check_vma=False)
```

time: 1860 us -> 404 us (0.22)
  waiting for transfers between devices: 1300 us -> 0 us
  matrix products: 443 us -> 0 us
  Pallas kernels: 0 us -> 395 us
  local copies, waits for them, and re-layouts: 62.5 us -> 8.6 us
  other arithmetic: 24.2 us -> 0 us
    reduce_scatter x6 -> x0, waiting for transfers between devices: 1030 us -> none  [body(): lax.psum_scatter(stacked, GRP, scatter_dimension=0, tiled=True)]
    dot_general x143 -> x0, matrix products: 443 us -> none  [the longest x48 171 us: dot_cols(): lax.dot_general(left, right, (((1,), (1,)), ((), ())), preferred_element_...]
    pallas_call x0 -> x2, Pallas kernels: none -> 395 us  [the longest x1 273 us: body(): pl.pallas_call(functools.partial(bwd_kernel, n_stage), name='backward', o...]
    all_gather x7 -> x0, waiting for transfers between devices: 273 us -> none  [the longest x6 273 us: whole(): full = lax.all_gather(w[v, 0], GRP, axis=0, tiled=True)]
    unnamed x489 -> x10, local copies, waits for them, and re-layouts: 55 us -> 8.6 us
  transfers between devices with their start and end apart: 13 -> 0, of which waited for: 11 -> 0; matrix products, arithmetic and copies ran while one was open for 12% -> 0% of each run, Pallas kernels for 0% -> 0%
where the time goes in v2:
time: 404 us
  Pallas kernels  395 us (98%)
  local copies, waits for them, and re-layouts  8.6 us (2%)
    pallas_call x1, Pallas kernels, body(): pl.pallas_call(functools.partial(bwd_kernel, n_stage), name='backward', o...  273 us
    pallas_call x1, Pallas kernels, body(): pl.pallas_call(functools.partial(fwd_kernel, n_stage), name='forward', ou...  121 us
    unnamed x10, local copies, waits for them, and re-layouts  8.6 us

profile of v2, /device:TPU:0, one launch (start us, length us, event | category | flops | bytes accessed | tf_op | source)
XLA Modules:
  0.0 404.0 jit_solution(2418034676929489992)
XLA Ops:
  0.6 121.5 %forward.1 = (bf16[16,3,2,2,64,1024]{5,4,3,2,1,0:T(8,128)(2,1)}, bf16[16,1536,256]{2,1,0:T(8,128)(2,1)}) custom-call(bf16[8,1536,256]{2,1,0:T(8,128)(2,1)} %bitcast.4, bf16[2,1,64,1024]{3,2,1,0:T(8,128)(2,1)} %wg.1, bf16[2,1,64,1024]{3,2,1,0:T(8,128)(2,1)} %wi.1, bf16[2,1,256,256]{3,2,1,0:T(8,128)(2,1)} %wo.1), custom_call_target="tpu_custom_call" | custom-call | flops 38654705664 | bytes 67108864 | tf_op jit(solution)/shard_map/forward/pallas_call | solution.py:507
  122.1 273.3 %backward.1 = (f32[2,1,64,1024]{3,2,1,0:T(8,128)}, f32[2,1,64,1024]{3,2,1,0:T(8,128)}, f32[2,1,256,256]{3,2,1,0:T(8,128)}, bf16[8,1536,256]{2,1,0:T(8,128)(2,1)}) custom-call(bf16[8,1536,256]{2,1,0:T(8,128)(2,1)} %bitcast.5, bf16[16,3,2,2,64,1024]{5,4,3,2,1,0:T(8,128)(2,1)} %get-tuple-element.10.w_all, bf16[16,1536,256]{2,1,0:T(8,128)(2,1)} %get-tuple-element.11.h_all), custom_call_target="tpu_custom_call" | custom-call | flops 103079215104 | bytes 67108864 | tf_op jit(solution)/shard_map/backward/pallas_call | solution.py:528
  395.4 0.0 copy-start.2
  395.4 0.0 copy-start.1
  395.4 0.0 copy-start
  395.4 6.2 %copy.13 = bf16[24,32,16,256]{3,2,1,0:T(8,128)(2,1)} copy(bf16[24,32,16,256]{3,2,1,0:T(8,128)(2,1)} %bitcast.3) | data formatting | bytes 12582912
  401.6 0.0 copy-done.2
  401.6 0.8 copy.14
  402.4 0.0 copy-done.1
  402.4 0.8 copy.15
  403.2 0.0 copy-done
  403.2 0.8 copy.16
Async XLA Ops:
  395.4 6.2 %copy-start.2 = (f32[2,1,64,1024]{3,2,1,0:T(8,128)S(1)}, f32[2,1,64,1024]{3,2,1,0:T(8,128)}, u32[]{:S(2)}) copy-start(f32[2,1,64,1024]{3,2,1,0:T(8,128)} %get-tuple-element.21) | copy-start | bytes 1572868
  395.4 7.0 %copy-start.1 = (f32[2,1,64,1024]{3,2,1,0:T(8,128)S(1)}, f32[2,1,64,1024]{3,2,1,0:T(8,128)}, u32[]{:S(2)}) copy-start(f32[2,1,64,1024]{3,2,1,0:T(8,128)} %get-tuple-element.22) | copy-start | bytes 1572868
  395.4 7.8 %copy-start = (f32[2,1,256,256]{3,2,1,0:T(8,128)S(1)}, f32[2,1,256,256]{3,2,1,0:T(8,128)}, u32[]{:S(2)}) copy-start(f32[2,1,256,256]{3,2,1,0:T(8,128)} %get-tuple-element.23) | copy-start | bytes 1572868

commit v3 on v2

--- a/solution.py
+++ b/solution.py
@@ -11,9 +11,12 @@
 MESH = pl.DeviceIdType.MESH
 SLOTS = 8
 FWD_LEAD = 7
-BWD_DRAIN = 8
+TICKS = 6
+Q_AT = (0, 6, 8, 18, 28, 39, 54)
+RELAY_AT = 22
 LANE, WIDE, HALF = 128, 256, 512
 PIECE, SUB = 64, 32
+LO, HI = slice(0, SUB), slice(SUB, PIECE)
 F32 = jnp.float32
 BF16 = jnp.bfloat16
 
@@ -227,13 +230,13 @@
     lax.fori_loop(0, n_block, drain, 0)
 
 
-def bwd_kernel(n_stage, cot, w_all, h_all, gg, gi, go, ga, w, h, e, g, x1, x2g, x2i, x2o, x3g, x3i, x3a, x3b, x4g, x4i, x4a, x4b, x5g, x5i, x5a, x5b, fg, fi, fa, fb, ssem, rsem, own, fsem, wsem, hsem, esem, a1s, a1r, a2s, a2r, a3s, a3r):
+def bwd_kernel(n_stage, cot, w_all, h_all, gg, gi, go, ga, w, h, e, g, x1, x2g, x2i, x2o, x3gl, x3il, x3gh, x3ih, x3a, x3b, x4g, x4i, x4a, x4b, x5g, x5i, x5a, x5b, fg, fi, fa, fb, ssem, rsem, own, fsem, wsem, hsem, esem, as_, ar, cs, cr, cl):
     here = Place()
     z, s, zn, zf, x, y, core = here.z, here.s, here.zn, here.zf, here.x, here.y, here.core
     n_block = w_all.shape[0]
     n_v = n_block // n_stage
     rows = h.shape[1]
-    tile = min(WIDE, rows // 2)
+    tile = rows // TICKS
     c_g, c_i = narrow(core, x, y), narrow(core, y, x)
 
     load_e = pltpu.make_async_copy(cot.at[s], e.at[s], esem)
@@ -302,10 +305,12 @@
                 x2i[q, f, k] += x1[q, 1, f, k, :, col(WIDE * y, WIDE)]
             x2o[q, f] += x1[q, 2, f, zn]
         push(3, b, (
-            (x2g.at[q, :, :, :, col(LANE - LANE * y, LANE)], x3g.at[q], here.to_y),
-            (x2i.at[q, :, :, :, col(LANE - LANE * x, LANE)], x3i.at[q], here.to_x),
-            (x2o.at[q, :, 0:SUB, col(WIDE - WIDE * x, WIDE)], x3a.at[q], here.to_x),
-            (x2o.at[q, :, SUB:PIECE, col(WIDE - WIDE * y, WIDE)], x3b.at[q], here.to_y),
+            (x2g.at[q, :, :, LO, col(LANE - LANE * y, LANE)], x3gl.at[q], here.to_y),
+            (x2i.at[q, :, :, LO, col(LANE - LANE * x, LANE)], x3il.at[q], here.to_x),
+            (x2g.at[q, :, 1 - zn, HI], x3gh.at[q], here.to_zn),
+            (x2i.at[q, :, 1 - zn, HI], x3ih.at[q], here.to_zn),
+            (x2o.at[q, :, LO, col(WIDE - WIDE * x, WIDE)], x3a.at[q], here.to_x),
+            (x2o.at[q, :, HI, col(WIDE - WIDE * y, WIDE)], x3b.at[q], here.to_y),
         ))
 
     def q4(b):
@@ -313,13 +318,17 @@
         q = b % SLOTS
         for f in range(2):
             for k in range(2):
-                x3g[q, f, k] += x2g[q, f, k, :, col(LANE * y, LANE)]
-                x3i[q, f, k] += x2i[q, f, k, :, col(LANE * x, LANE)]
-            x3a[q, f] += x2o[q, f, 0:SUB, col(WIDE * x, WIDE)]
-            x3b[q, f] += x2o[q, f, SUB:PIECE, col(WIDE * y, WIDE)]
+                x3gl[q, f, k] += x2g[q, f, k, LO, col(LANE * y, LANE)]
+                x3il[q, f, k] += x2i[q, f, k, LO, col(LANE * x, LANE)]
+            x3gh[q, f] += x2g[q, f, zn, HI]
+            x3ih[q, f] += x2i[q, f, zn, HI]
+            x3a[q, f] += x2o[q, f, LO, col(WIDE * x, WIDE)]
+            x3b[q, f] += x2o[q, f, HI, col(WIDE * y, WIDE)]
         push(4, b, (
-            (x3g.at[q, :, 1 - zn], x4g.at[q], here.to_zn),
-            (x3i.at[q, :, 1 - zn], x4i.at[q], here.to_zn),
+            (x3gl.at[q, :, 1 - zn], x4g.at[q, :, LO], here.to_zn),
+            (x3il.at[q, :, 1 - zn], x4i.at[q, :, LO], here.to_zn),
+            (x3gh.at[q, :, :, col(LANE - LANE * y, LANE)], x4g.at[q, :, HI], here.to_y),
+            (x3ih.at[q, :, :, col(LANE - LANE * x, LANE)], x4i.at[q, :, HI], here.to_x),
             (x3a.at[q, :, :, col(LANE - LANE * y, LANE)], x4a.at[q], here.to_y),
             (x3b.at[q, :, :, col(LANE - LANE * x, LANE)], x4b.at[q], here.to_x),
         ))
@@ -328,8 +337,10 @@
         taken(4, b)
         q = b % SLOTS
         for f in range(2):
-            x4g[q, f] += x3g[q, f, zn]
-            x4i[q, f] += x3i[q, f, zn]
+            x4g[q, f, LO] += x3gl[q, f, zn]
+            x4i[q, f, LO] += x3il[q, f, zn]
+            x4g[q, f, HI] += x3gh[q, f, :, col(LANE * y, LANE)]
+            x4i[q, f, HI] += x3ih[q, f, :, col(LANE * x, LANE)]
             x4a[q, f] += x3a[q, f, :, col(LANE * y, LANE)]
             x4b[q, f] += x3b[q, f, :, col(LANE * x, LANE)]
         push(5, b, (
@@ -403,75 +414,77 @@
         grad = et.astype(F32) + inv * (q - hr * jnp.mean(q * hr, axis=-1, keepdims=True))
         e[s, at, :] = grad.astype(BF16)
 
-    per_half = rows // tile // 2
-
-    def half_step(i, carry):
-        b = i // 2
-
-        @pl.when(i % 2 == 0)
-        def _():
-            when_valid(b - 8, q6)
-            when_valid(b - 5, q4)
-            when_valid(b - 2, q2)
-
-            @pl.when(b < n_block)
+    def step(i, carry):
+        for k, fn in ((6, q6), (5, q5), (4, q4), (3, q3), (2, q2), (1, q1)):
+            since = i - Q_AT[k]
+
+            @pl.when((since >= 0) & (since < TICKS * n_block) & ((since + TICKS * n_block) % TICKS == 0))
+            def _(fn=fn, since=since):
+                fn(since // TICKS)
+
+        @pl.when(i < TICKS * n_block)
+        def _():
+            b = i // TICKS
+
+            @pl.when(i % TICKS == 0)
             def _():
                 for copy in fetch(b):
                     copy.wait()
 
-            @pl.when(b + 1 < n_block)
-            def _():
-                for copy in fetch(b + 1):
-                    copy.start()
-
-        @pl.when(i % 2 == 1)
-        def _():
-            when_valid(b - 6, q5)
-            when_valid(b - 3, q3)
-
-        @pl.when(b < n_block)
-        def _():
-            def body(j, carry):
-                one_tile(b, (i % 2) * per_half + j)
-                return carry
-
-            lax.fori_loop(0, per_half, body, 0)
-
-            @pl.when(i % 2 == 1)
-            def _():
-                q1(b)
+                @pl.when(b + 1 < n_block)
+                def _():
+                    for copy in fetch(b + 1):
+                        copy.start()
+
+            one_tile(b, i % TICKS)
 
         return carry
-
-    lax.fori_loop(0, 2 * n_block, half_step, 0)
 
     half = rows // 2
     lo, hi = pl.ds(0, half), pl.ds(half, half)
     sx, sy = here.to_x[1], here.to_y[1]
-    first = [remote(e.at[s, lo], e.at[s, lo], a1s.at[0], a1r.at[0], here.to_x), remote(e.at[s, hi], e.at[s, hi], a1s.at[1], a1r.at[1], here.to_y)]
-    for copy in first:
+    sd = 2 * ((sx // 2 + sy // 2 - s // 2) % (n_stage // 2)) + core
+
+    def share(k, slot, part, to):
+        return remote(e.at[slot, part], e.at[slot, part], as_.at[k], ar.at[k], to)
+
+    first = (share(0, s, lo, here.to_x), share(1, s, lo, here.to_y), share(2, s, hi, here.to_y), share(3, s, hi, here.to_x))
+    relay = (share(4, sx, lo, here.to_y), share(5, sy, hi, here.to_x))
+
+    def hand(k, slot):
+        return (
+            remote(e.at[slot], ga.at[slot], cs.at[k], cr.at[k], here.to_core),
+            pltpu.make_async_copy(e.at[slot], ga.at[slot], cl.at[k]),
+        )
+
+    hands = [hand(k, slot) for k, slot in enumerate((s, sx, sy, sd))]
+    last = TICKS * n_block
+    lax.fori_loop(0, last - TICKS // 2, step, 0)
+    for copy in first[:2]:
         copy.start()
-    lax.fori_loop(2 * n_block, 2 * n_block + 4, half_step, 0)
-    for copy in first:
-        copy.wait()
-    second = [
-        remote(e.at[s, lo], e.at[s, lo], a2s.at[0], a2r.at[0], here.to_y),
-        remote(e.at[sx, lo], e.at[sx, lo], a2s.at[1], a2r.at[1], here.to_y),
-        remote(e.at[s, hi], e.at[s, hi], a2s.at[2], a2r.at[2], here.to_x),
-        remote(e.at[sy, hi], e.at[sy, hi], a2s.at[3], a2r.at[3], here.to_x),
-    ]
-    for copy in second:
+    lax.fori_loop(last - TICKS // 2, last, step, 0)
+    for copy in first[2:]:
         copy.start()
-    lax.fori_loop(2 * n_block + 4, 2 * (n_block + BWD_DRAIN) + 1, half_step, 0)
-    for copy in second:
-        copy.wait()
-    last = []
-    for k in range(n_stage // 2):
-        q = 2 * k + core
-        last.append(remote(e.at[q], ga.at[q], a3s.at[k], a3r.at[k], here.to_core))
-        last.append(pltpu.make_async_copy(e.at[q], ga.at[q], a3s.at[n_stage // 2 + k]))
-    for copy in last:
+    lax.fori_loop(last, last + RELAY_AT, step, 0)
+    first[0].wait_recv()
+    relay[0].start()
+    first[2].wait_recv()
+    relay[1].start()
+    for copy in hands[0]:
         copy.start()
+    lax.fori_loop(last + RELAY_AT, last + Q_AT[6], step, 0)
+    first[3].wait_recv()
+    for copy in hands[1]:
+        copy.start()
+    first[1].wait_recv()
+    for copy in hands[2]:
+        copy.start()
+    for copy in relay:
+        copy.wait_recv()
+    for copy in hands[3]:
+        copy.start()
+    for copy in first + relay:
+        copy.wait_send()
 
     def finish(b, carry):
         wait_bytes(total(5, 0), own.at[b])
@@ -480,8 +493,29 @@
     lax.fori_loop(0, n_block, finish, 0)
     for v in range(n_v):
         wait_bytes(g.at[0, :, 0, 0, :, 0 : LANE * (n_stage - 1)], fsem.at[v])
-    for copy in last:
-        copy.wait()
+    for pair in hands:
+        for copy in pair:
+            copy.wait()
+
+
+def settle_kernel(*refs):
+    n = (len(refs) - 2) // 3
+    srcs, dsts, bufs, (rsem, wsem) = refs[:n], refs[n : 2 * n], refs[2 * n : 3 * n], refs[3 * n :]
+    moves = []
+    for a in range(n):
+        for i in range(srcs[a].shape[0]):
+            k = len(moves)
+            moves.append((
+                pltpu.make_async_copy(srcs[a].at[i], bufs[a].at[i], rsem.at[k]),
+                pltpu.make_async_copy(bufs[a].at[i], dsts[a].at[i], wsem.at[k]),
+            ))
+    for read, _ in moves:
+        read.start()
+    for read, write in moves:
+        read.wait()
+        write.start()
+    for _, write in moves:
+        write.wait()
 
 
 def solution(mesh):
@@ -545,8 +579,10 @@
                 f32(n, 2, 2, PIECE, WIDE),
                 f32(n, 2, 2, PIECE, WIDE),
                 f32(n, 2, PIECE, HALF),
-                f32(n, 2, 2, PIECE, LANE),
-                f32(n, 2, 2, PIECE, LANE),
+                f32(n, 2, 2, SUB, LANE),
+                f32(n, 2, 2, SUB, LANE),
+                f32(n, 2, SUB, WIDE),
+                f32(n, 2, SUB, WIDE),
                 f32(n, 2, SUB, WIDE),
                 f32(n, 2, SUB, WIDE),
                 f32(n, 2, PIECE, LANE),
@@ -568,16 +604,25 @@
                 dma((2,)),
                 dma((2,)),
                 dma,
-                dma((2,)),
-                dma((2,)),
+                dma((TICKS,)),
+                dma((TICKS,)),
                 dma((4,)),
                 dma((4,)),
-                dma((n_stage,)),
-                dma((n_stage // 2,)),
+                dma((4,)),
             ],
             compiler_params=pltpu.CompilerParams(collective_id=1, has_side_effects=True, vmem_limit_bytes=63 * 2**20),
             cost_estimate=pl.CostEstimate(flops=8 * flops, bytes_accessed=2**26, transcendentals=0),
         )(cot, w_all, h_all)
+        done = (ga, gg, gi, go)
+        moved = sum(a.shape[0] for a in done)
+        ga, gg, gi, go = pl.pallas_call(
+            settle_kernel,
+            name="settle",
+            out_shape=[jax.ShapeDtypeStruct(a.shape, a.dtype) for a in done],
+            in_specs=[hbm] * 4,
+            out_specs=[hbm] * 4,
+            scratch_shapes=[pltpu.VMEM(a.shape, a.dtype) for a in done] + [dma((moved,)), dma((moved,))],
+        )(*done)
         return ga.reshape(act_in.shape), gg, gi, go
 
     return jax.shard_map(body, mesh=mesh, in_specs=(act_spec, act_spec, w_spec, w_spec, w_spec), out_specs=(act_spec, w_spec, w_spec, w_spec), check_vma=False)

time: 404 us -> 402 us (level)
  local copies, waits for them, and re-layouts: 8.6 us -> 0 us
  Pallas kernels: 395 us -> 401 us
    unnamed x10 -> x0, local copies, waits for them, and re-layouts: 8.6 us -> none
    pallas_call x0 -> x1, Pallas kernels: none -> 6.12 us  [body(): pl.pallas_call(settle_kernel, name='settle', out_shape=[jax.ShapeDtypeStr...]
where the time goes in v3:
time: 402 us
  Pallas kernels  401 us (100%)
    pallas_call x1, Pallas kernels, body(): pl.pallas_call(functools.partial(bwd_kernel, n_stage), name='backward', o...  274 us
    pallas_call x1, Pallas kernels, body(): pl.pallas_call(functools.partial(fwd_kernel, n_stage), name='forward', ou...  121 us

profile of v3, /device:TPU:0, one launch (start us, length us, event | category | flops | bytes accessed | tf_op | source)
XLA Modules:
  0.0 402.0 jit_solution(17306454271471600337)
XLA Ops:
  0.6 121.5 %forward.1 = (bf16[16,3,2,2,64,1024]{5,4,3,2,1,0:T(8,128)(2,1)}, bf16[16,1536,256]{2,1,0:T(8,128)(2,1)}) custom-call(bf16[8,1536,256]{2,1,0:T(8,128)(2,1)} %bitcast.3, bf16[2,1,64,1024]{3,2,1,0:T(8,128)(2,1)} %wg.1, bf16[2,1,64,1024]{3,2,1,0:T(8,128)(2,1)} %wi.1, bf16[2,1,256,256]{3,2,1,0:T(8,128)(2,1)} %wo.1), custom_call_target="tpu_custom_call" | custom-call | flops 38654705664 | bytes 67108864 | tf_op jit(solution)/shard_map/forward/pallas_call | solution.py:541
  122.1 273.7 %backward.1 = (f32[2,1,64,1024]{3,2,1,0:T(8,128)}, f32[2,1,64,1024]{3,2,1,0:T(8,128)}, f32[2,1,256,256]{3,2,1,0:T(8,128)}, bf16[8,1536,256]{2,1,0:T(8,128)(2,1)}) custom-call(bf16[8,1536,256]{2,1,0:T(8,128)(2,1)} %bitcast.4, bf16[16,3,2,2,64,1024]{5,4,3,2,1,0:T(8,128)(2,1)} %get-tuple-element.14.w_all, bf16[16,1536,256]{2,1,0:T(8,128)(2,1)} %get-tuple-element.15.h_all), custom_call_target="tpu_custom_call" | custom-call | flops 103079215104 | bytes 67108864 | tf_op jit(solution)/shard_map/backward/pallas_call | solution.py:562
  395.8 6.1 %settle.1 = (bf16[8,1536,256]{2,1,0:T(8,128)(2,1)}, f32[2,1,64,1024]{3,2,1,0:T(8,128)}, f32[2,1,64,1024]{3,2,1,0:T(8,128)}, f32[2,1,256,256]{3,2,1,0:T(8,128)}) custom-call(bf16[8,1536,256]{2,1,0:T(8,128)(2,1)} %get-tuple-element.16.refs_0_, f32[2,1,64,1024]{3,2,1,0:T(8,128)} %get-tuple-element.17.refs_1_, f32[2,1,64,1024]{3,2,1,0:T(8,128)} %get-tuple-element.18.refs_2_, ...), custom_call_target="tpu_custom_call" | custom-call | tf_op jit(solution)/shard_map/settle/pallas_call | solution.py:618

commit v4 on v3

--- a/solution.py
+++ b/solution.py
@@ -9,11 +9,11 @@
 
 NORM_EPS = 1e-6
 MESH = pl.DeviceIdType.MESH
-SLOTS = 8
-FWD_LEAD = 7
-TICKS = 6
-Q_AT = (0, 6, 8, 18, 28, 39, 54)
-RELAY_AT = 22
+SLOTS = 10
+TICKS = 3
+P_AHEAD = (0, 19, 14, 10, 5, 2)
+Q_AT = (0, 3, 5, 10, 19, 27, 37)
+RELAY_AT = 20
 LANE, WIDE, HALF = 128, 256, 512
 PIECE, SUB = 64, 32
 LO, HI = slice(0, SUB), slice(SUB, PIECE)
@@ -83,7 +83,7 @@
     n_block = w.shape[0]
     n_v = n_block // n_stage
     rows = h.shape[1]
-    tile = min(WIDE, rows // 2)
+    tile = rows // TICKS
     c_g, c_i = narrow(here.core, here.x, here.y), narrow(here.core, here.y, here.x)
     c_x, c_y, c_c = narrow(here.core, here.x, 0), narrow(here.core, here.y, 0), narrow(here.core, 0, 0)
 
@@ -158,12 +158,10 @@
             wait_bytes(total(phase, c), ssem.at[phase - 1, slot])
 
     def advance(phase, c):
-        @pl.when((c >= 0) & (c < n_block))
-        def _():
-            arrived(phase - 1, c)
-            slot = c % SLOTS
-            for ref, to in parts(phase, c):
-                remote(ref, ref, ssem.at[phase - 1, slot], rsem.at[phase - 1, slot], to).start()
+        arrived(phase - 1, c)
+        slot = c % SLOTS
+        for ref, to in parts(phase, c):
+            remote(ref, ref, ssem.at[phase - 1, slot], rsem.at[phase - 1, slot], to).start()
 
     def one_tile(c, i):
         at = pl.ds(pl.multiple_of(i * tile, tile), tile)
@@ -171,54 +169,48 @@
         inv = lax.rsqrt(jnp.mean(x32 * x32, axis=-1, keepdims=True) + NORM_EPS)
         n = (x32 * inv).astype(BF16)
         acc = x32
+        ahead = mat(n, square(w, c, 0, 0)), mat(n, square(w, c, 1, 0))
         for k in range(4):
-            a = mat(n, square(w, c, 0, k))
-            b = mat(n, square(w, c, 1, k))
+            a, b = ahead
+            if k < 3:
+                ahead = mat(n, square(w, c, 0, k + 1)), mat(n, square(w, c, 1, k + 1))
             u = (a * jax.nn.sigmoid(a) * b).astype(BF16)
             acc += mat(u, out_square(w, c, k))
         h[c + 1, at, :] = acc.astype(BF16)
 
-    per_half = rows // tile // 2
-
-    def half_step(i, carry):
-        c = i // 2 - FWD_LEAD
-        second = i % 2 == 1
-
-        @pl.when(i % 2 == 0)
+    lead = max(P_AHEAD)
+
+    def step(i, carry):
+        for k in (5, 4, 3, 2, 1):
+            since = i - lead + P_AHEAD[k]
+
+            @pl.when((since >= 0) & (since < TICKS * n_block) & ((since + TICKS * lead) % TICKS == 0))
+            def _(k=k, since=since):
+                advance(k, since // TICKS)
+
+        @pl.when(i >= lead)
         def _():
-            advance(4, c + 2)
-            advance(2, c + 5)
-
-            @pl.when(c == 0)
-            def _():
-                load.wait()
-
-            @pl.when(c >= 0)
+            now = i - lead
+            c = now // TICKS
+
+            @pl.when(now % TICKS == 0)
             def _():
                 arrived(5, c)
 
-        @pl.when(second)
-        def _():
-            advance(5, c + 1)
-            advance(3, c + 4)
-            advance(1, c + 7)
-
-            @pl.when(c >= 0)
+            @pl.when(now % TICKS == 1)
             def _():
                 pltpu.make_async_copy(w.at[c], w_all.at[c], wsem.at[c]).start()
                 pltpu.make_async_copy(h.at[c], h_all.at[c], hsem.at[c]).start()
 
-        @pl.when((c >= 0) & (c < n_block - 1))
-        def _():
-            def body(j, carry):
-                one_tile(c, (i % 2) * per_half + j)
-                return carry
-
-            lax.fori_loop(0, per_half, body, 0)
+            @pl.when(c < n_block - 1)
+            def _():
+                one_tile(c, now % TICKS)
 
         return carry
 
-    lax.fori_loop(0, 2 * (n_block + FWD_LEAD), half_step, 0)
+    lax.fori_loop(0, lead, step, 0)
+    load.wait()
+    lax.fori_loop(lead, lead + TICKS * n_block, step, 0)
     for v in range(n_v):
         wait_bytes(w.at[0, :, 0, 0, :, 0 : LANE * (n_stage - 1)], s0.at[v])
 
@@ -394,17 +386,20 @@
                     old = g[p, m, f, r, :, WIDE * k : WIDE * k + WIDE]
                     g[p, m, f, r, :, WIDE * k : WIDE * k + WIDE] = part + jnp.where(first, 0.0, old)
 
+        def up(k):
+            return mat(n, square(w, p, 0, k)), mat(n, square(w, p, 1, k)), mat_cols(et, out_square(w, p, k))
+
+        ahead = up(0)
         for k in range(4):
-            wg, wi, wo = square(w, p, 0, k), square(w, p, 1, k), out_square(w, p, k)
-            a = mat(n, wg)
-            bb = mat(n, wi)
-            t = mat_cols(et, wo)
+            a, bb, t = ahead
+            if k < 3:
+                ahead = up(k + 1)
             sg = jax.nn.sigmoid(a)
             act = a * sg
             u = (act * bb).astype(BF16)
             da = (t * bb * sg * (1.0 + a * (1.0 - sg))).astype(BF16)
             db = (t * act).astype(BF16)
-            q += mat_cols(da, wg) + mat_cols(db, wi)
+            q += mat_cols(da, square(w, p, 0, k)) + mat_cols(db, square(w, p, 1, k))
             add(0, k, mat_rows(n, da))
             add(1, k, mat_rows(n, db))
             do = mat_rows(u, et)
@@ -459,10 +454,10 @@
 
     hands = [hand(k, slot) for k, slot in enumerate((s, sx, sy, sd))]
     last = TICKS * n_block
-    lax.fori_loop(0, last - TICKS // 2, step, 0)
+    lax.fori_loop(0, last - 1, step, 0)
     for copy in first[:2]:
         copy.start()
-    lax.fori_loop(last - TICKS // 2, last, step, 0)
+    lax.fori_loop(last - 1, last, step, 0)
     for copy in first[2:]:
         copy.start()
     lax.fori_loop(last, last + RELAY_AT, step, 0)
@@ -604,8 +599,8 @@
                 dma((2,)),
                 dma((2,)),
                 dma,
-                dma((TICKS,)),
-                dma((TICKS,)),
+                dma((6,)),
+                dma((6,)),
                 dma((4,)),
                 dma((4,)),
                 dma((4,)),

time: 402 us -> 352 us (0.88)
  Pallas kernels: 401 us -> 351 us
    pallas_call x1, Pallas kernels: 274 us -> 229 us  [body(): pl.pallas_call(functools.partial(bwd_kernel, n_stage), name='backward', o...]
    pallas_call x1, Pallas kernels: 121 us -> 116 us  [body(): pl.pallas_call(functools.partial(fwd_kernel, n_stage), name='forward', ou...]
where the time goes in v4:
time: 352 us; the launch traced here: 351 us
  Pallas kernels  351 us (100%)
    pallas_call x1, Pallas kernels, body(): pl.pallas_call(functools.partial(bwd_kernel, n_stage), name='backward', o...  229 us
    pallas_call x1, Pallas kernels, body(): pl.pallas_call(functools.partial(fwd_kernel, n_stage), name='forward', ou...  116 us

profile of v4, /device:TPU:0, one launch (start us, length us, event | category | flops | bytes accessed | tf_op | source)
XLA Modules:
  0.0 351.4 jit_solution(12899165682595216531)
XLA Ops:
  0.6 115.6 %forward.1 = (bf16[16,3,2,2,64,1024]{5,4,3,2,1,0:T(8,128)(2,1)}, bf16[16,1536,256]{2,1,0:T(8,128)(2,1)}) custom-call(bf16[8,1536,256]{2,1,0:T(8,128)(2,1)} %bitcast.3, bf16[2,1,64,1024]{3,2,1,0:T(8,128)(2,1)} %wg.1, bf16[2,1,64,1024]{3,2,1,0:T(8,128)(2,1)} %wi.1, bf16[2,1,256,256]{3,2,1,0:T(8,128)(2,1)} %wo.1), custom_call_target="tpu_custom_call" | custom-call | flops 38654705664 | bytes 67108864 | tf_op jit(solution)/shard_map/forward/pallas_call | solution.py:536
  116.3 228.8 %backward.1 = (f32[2,1,64,1024]{3,2,1,0:T(8,128)}, f32[2,1,64,1024]{3,2,1,0:T(8,128)}, f32[2,1,256,256]{3,2,1,0:T(8,128)}, bf16[8,1536,256]{2,1,0:T(8,128)(2,1)}) custom-call(bf16[8,1536,256]{2,1,0:T(8,128)(2,1)} %bitcast.4, bf16[16,3,2,2,64,1024]{5,4,3,2,1,0:T(8,128)(2,1)} %get-tuple-element.14.w_all, bf16[16,1536,256]{2,1,0:T(8,128)(2,1)} %get-tuple-element.15.h_all), custom_call_target="tpu_custom_call" | custom-call | flops 103079215104 | bytes 67108864 | tf_op jit(solution)/shard_map/backward/pallas_call | solution.py:557
  345.1 6.1 %settle.1 = (bf16[8,1536,256]{2,1,0:T(8,128)(2,1)}, f32[2,1,64,1024]{3,2,1,0:T(8,128)}, f32[2,1,64,1024]{3,2,1,0:T(8,128)}, f32[2,1,256,256]{3,2,1,0:T(8,128)}) custom-call(bf16[8,1536,256]{2,1,0:T(8,128)(2,1)} %get-tuple-element.16.refs_0_, f32[2,1,64,1024]{3,2,1,0:T(8,128)} %get-tuple-element.17.refs_1_, f32[2,1,64,1024]{3,2,1,0:T(8,128)} %get-tuple-element.18.refs_2_, ...), custom_call_target="tpu_custom_call" | custom-call | tf_op jit(solution)/shard_map/settle/pallas_call | solution.py:613

commit v5 on v4

v5 whole, which is shorter than its diff:
```python
import functools

import jax
import jax.numpy as jnp
from jax import lax
from jax.experimental import pallas as pl
from jax.experimental.pallas import tpu as pltpu
from jax.sharding import PartitionSpec as P

NORM_EPS = 1e-6
MESH = pl.DeviceIdType.MESH
TICKS = 3
H_SLOTS = 3
F_SLOTS = 6
P_SLOTS = 10
P_AHEAD = (0, 20, 15, 11, 6, 3)
Q_SLOTS = (0, 4, 7, 9, 9, 8)
Q_AT = (0, 3, 5, 10, 18, 26, 36)
SHARE_AT = (-1, 0, 2, 3, 17, 20)
LANE, WIDE, HALF = 128, 256, 512
PIECE, SUB = 64, 32
LO, HI = slice(0, SUB), slice(SUB, PIECE)
F32 = jnp.float32
BF16 = jnp.bfloat16


class Place:
    def __init__(self):
        self.z, self.s = lax.axis_index("data"), lax.axis_index("stage")
        self.core, self.x, self.y = self.s % 2, (self.s // 2) % 2, self.s // 4
        self.zn, self.zf = self.z % 2, self.z // 2
        self.to_x = (self.z, self.s + 2 - 4 * self.x)
        self.to_y = (self.z, self.s + 4 - 8 * self.y)
        self.to_core = (self.z, self.s + 1 - 2 * self.core)
        self.to_zn = (self.z + 1 - 2 * self.zn, self.s)
        self.to_zf = (self.z + 2 - 4 * self.zf, self.s)


def col(start, size):
    return pl.ds(pl.multiple_of(start, LANE), size)


def narrow(core, hi, lo):
    return HALF * core + WIDE * hi + LANE * lo


def remote(src, dst, ssem, rsem, to):
    return pltpu.make_async_remote_copy(src_ref=src, dst_ref=dst, send_sem=ssem, recv_sem=rsem, device_id=to, device_id_type=MESH)


def wait_bytes(ref, sem):
    pltpu.make_async_copy(ref, ref, sem).wait()


def enter(here, n_stage):
    barrier = pltpu.get_barrier_semaphore()
    peers = [(here.z, (here.s + k) % n_stage) for k in range(1, n_stage)] + [here.to_zn, here.to_zf]
    for peer in peers:
        pl.semaphore_signal(barrier, inc=1, device_id=peer, device_id_type=MESH)
    pl.semaphore_wait(barrier, len(peers))


def mat_rows(left, right):
    return lax.dot_general(left, right, (((0,), (0,)), ((), ())), preferred_element_type=F32)


def mat_cols(left, right):
    return lax.dot_general(left, right, (((1,), (1,)), ((), ())), preferred_element_type=F32)


def mat(left, right):
    return jnp.dot(left, right, preferred_element_type=F32)


def square(w_ref, at, m, k):
    return w_ref[at, m, :, :, :, WIDE * k : WIDE * k + WIDE].reshape(WIDE, WIDE)


def out_square(w_ref, at, k):
    return jnp.concatenate([w_ref[at, 2, k // 2, k % 2, :, WIDE * j : WIDE * j + WIDE] for j in range(4)], axis=0)


def step_kernel(n_stage, act, cot, wg, wi, wo, gg, gi, go, ga, h_all, w, h, e, g, x1, x2g, x2i, x2o, x3gl, x3il, x3gh, x3ih, x3a, x3b, x4g, x4i, x4a, x4b, x5g, x5i, x5a, x5b, fg, fi, fa, fb, s0, r0, ps, pr, qs, qr, own, fsem, hsem, esem, as_, ar, cs, cr, cl):
    here = Place()
    z, s, zn, zf, x, y, core = here.z, here.s, here.zn, here.zf, here.x, here.y, here.core
    n_block = w.shape[0]
    n_v = n_block // n_stage
    rows = h.shape[1]
    tile = rows // TICKS
    span = TICKS * n_block
    c_g, c_i = narrow(core, x, y), narrow(core, y, x)
    c_x, c_y, c_c = narrow(core, x, 0), narrow(core, y, 0), narrow(core, 0, 0)

    enter(here, n_stage)
    load_h = pltpu.make_async_copy(act.at[s], h.at[0], esem.at[0])
    load_e = pltpu.make_async_copy(cot.at[s], e.at[0], esem.at[1])
    load_h.start()

    def scatter(v, k):
        q = (s + k) % n_stage
        core, x, y = q % 2, (q // 2) % 2, q // 4
        d_g, d_i = narrow(core, x, y), narrow(core, y, x)
        c = v * n_stage + s
        moves = (
            (wg.at[v, 0, :, col(d_g, LANE)], w.at[c, 0, zf, zn, :, col(d_g, LANE)]),
            (wi.at[v, 0, :, col(d_i, LANE)], w.at[c, 1, zf, zn, :, col(d_i, LANE)]),
            (wo.at[v, 0, pl.ds(pl.multiple_of(PIECE * (2 * core + x), SUB), SUB), col(LANE * y, LANE)], w.at[c, 2, zf, zn, 0:SUB, col(d_g, LANE)]),
            (wo.at[v, 0, pl.ds(pl.multiple_of(PIECE * (2 * core + y) + SUB, SUB), SUB), col(LANE * x, LANE)], w.at[c, 2, zf, zn, SUB:PIECE, col(d_i, LANE)]),
        )
        for src, dst in moves:
            if k == 0:
                pltpu.make_async_copy(src, dst, r0.at[c]).start()
            else:
                remote(src, dst, s0.at[v], r0.at[c], (z, q)).start()

    for v in range(n_v):
        for k in range(n_stage):
            scatter(v, k)
    load_e.start()

    def parts(phase, c):
        if phase == 1:
            return (
                (w.at[c, 0, zf, zn, :, col(c_g, LANE)], here.to_zf),
                (w.at[c, 1, zf, zn, :, col(c_i, LANE)], here.to_zf),
                (w.at[c, 2, zf, zn, 0:SUB, col(c_g, LANE)], here.to_zf),
                (w.at[c, 2, zf, zn, SUB:PIECE, col(c_i, LANE)], here.to_zf),
            )
        if phase == 2:
            return (
                (w.at[c, 0, :, zn, :, col(c_g, LANE)], here.to_zn),
                (w.at[c, 1, :, zn, :, col(c_i, LANE)], here.to_zn),
                (w.at[c, 2, :, zn, 0:SUB, col(c_g, LANE)], here.to_y),
                (w.at[c, 2, :, zn, SUB:PIECE, col(c_i, LANE)], here.to_x),
            )
        if phase == 3:
            return (
                (w.at[c, 0, :, :, :, col(c_g, LANE)], here.to_y),
                (w.at[c, 1, :, :, :, col(c_i, LANE)], here.to_x),
                (w.at[c, 2, :, zn, 0:SUB, col(c_x, WIDE)], here.to_x),
                (w.at[c, 2, :, zn, SUB:PIECE, col(c_y, WIDE)], here.to_y),
            )
        if phase == 4:
            return (
                (w.at[c, 0, :, :, :, col(c_x, WIDE)], here.to_x),
                (w.at[c, 1, :, :, :, col(c_y, WIDE)], here.to_y),
                (w.at[c, 2, :, zn, :, col(c_c, HALF)], here.to_zn),
            )
        return ((w.at[c, :, :, :, :, col(c_c, HALF)], here.to_core),)

    def w_total(phase, c):
        if phase == 1:
            return w.at[c, :, 0, 0, :, 0:LANE]
        if phase == 2:
            return w.at[c, :, :, 0, :, 0:LANE]
        return w.at[c, :, :, :, :, 0 : {3: LANE, 4: WIDE, 5: HALF}[phase]]

    def arrived(phase, c):
        if phase == 0:
            wait_bytes(w_total(1, c), r0.at[c])
        else:
            slot = c % P_SLOTS
            wait_bytes(w_total(phase, c), pr.at[phase - 1, slot])
            wait_bytes(w_total(phase, c), ps.at[phase - 1, slot])

    def advance(phase, c):
        arrived(phase - 1, c)
        slot = c % P_SLOTS
        for ref, to in parts(phase, c):
            remote(ref, ref, ps.at[phase - 1, slot], pr.at[phase - 1, slot], to).start()

    def fwd_tile(c, i):
        at = pl.ds(pl.multiple_of(i * tile, tile), tile)
        x32 = h[c % H_SLOTS, at, :].astype(F32)
        inv = lax.rsqrt(jnp.mean(x32 * x32, axis=-1, keepdims=True) + NORM_EPS)
        n = (x32 * inv).astype(BF16)
        acc = x32
        ahead = mat(n, square(w, c, 0, 0)), mat(n, square(w, c, 1, 0))
        for k in range(4):
            a, b = ahead
            if k < 3:
                ahead = mat(n, square(w, c, 0, k + 1)), mat(n, square(w, c, 1, k + 1))
            u = (a * jax.nn.sigmoid(a) * b).astype(BF16)
            acc += mat(u, out_square(w, c, k))
        h[(c + 1) % H_SLOTS, at, :] = acc.astype(BF16)

    def keep(c):
        return pltpu.make_async_copy(h.at[c % H_SLOTS], h_all.at[c], hsem.at[c])

    def recall(c):
        return pltpu.make_async_copy(h_all.at[c], h.at[c % H_SLOTS], hsem.at[c])

    n_kept = n_block - H_SLOTS
    lead = max(P_AHEAD)

    def lead_step(i, carry):
        for k in (5, 4, 3, 2, 1):
            since = i - lead + P_AHEAD[k]

            @pl.when((since >= 0) & (since < span) & ((since + TICKS * lead) % TICKS == 0))
            def _(k=k, since=since):
                advance(k, since // TICKS)

        return carry

    def fwd_step(i, carry):
        lead_step(i, carry)
        now = i - lead
        c = now // TICKS

        @pl.when(now % TICKS == 0)
        def _():
            arrived(5, c)

            @pl.when((c >= 2) & (c - 2 < n_kept))
            def _():
                keep(c - 2).wait()

        @pl.when((now % TICKS == 1) & (c < n_kept))
        def _():
            keep(c).start()

        @pl.when(c < n_block - 1)
        def _():
            fwd_tile(c, now % TICKS)

        return carry

    lax.fori_loop(0, lead, lead_step, 0)
    load_h.wait()
    lax.fori_loop(lead, lead + span, fwd_step, 0)
    load_e.wait()

    def g_total(phase):
        if phase == 1:
            return x1.at[0]
        if phase == 2:
            return x1.at[0, :, :, :, :, 0:WIDE]
        if phase == 3:
            return x1.at[0, :, :, :, :, 0:LANE]
        if phase == 4:
            return x1.at[0, :, :, 0, :, 0:LANE]
        return x1.at[0, :, 0, 0, :, 0:LANE]

    def slot_of(phase, b):
        return b % Q_SLOTS[phase]

    def push(phase, b, moves):
        slot = slot_of(phase, b)
        for src, dst, to in moves:
            remote(src, dst, qs.at[phase - 1, slot], qr.at[phase - 1, slot], to).start()

    def taken(phase, b):
        slot = slot_of(phase, b)
        wait_bytes(g_total(phase), qr.at[phase - 1, slot])
        wait_bytes(g_total(phase), qs.at[phase - 1, slot])

    def q1(b):
        push(1, b, ((g.at[b % 2, :, :, :, :, col(HALF - HALF * core, HALF)], x1.at[slot_of(1, b)], here.to_core),))

    def q2(b):
        taken(1, b)
        q, t, p = slot_of(1, b), slot_of(2, b), b % 2
        for m in range(3):
            for f in range(2):
                for k in range(2):
                    x1[q, m, f, k] += g[p, m, f, k, :, col(HALF * core, HALF)]
        push(2, b, (
            (x1.at[q, 0, :, :, :, col(WIDE - WIDE * x, WIDE)], x2g.at[t], here.to_x),
            (x1.at[q, 1, :, :, :, col(WIDE - WIDE * y, WIDE)], x2i.at[t], here.to_y),
            (x1.at[q, 2, :, 1 - zn], x2o.at[t], here.to_zn),
        ))

    def q3(b):
        taken(2, b)
        o, q, t = slot_of(1, b), slot_of(2, b), slot_of(3, b)
        for f in range(2):
            for k in range(2):
                x2g[q, f, k] += x1[o, 0, f, k, :, col(WIDE * x, WIDE)]
                x2i[q, f, k] += x1[o, 1, f, k, :, col(WIDE * y, WIDE)]
            x2o[q, f] += x1[o, 2, f, zn]
        push(3, b, (
            (x2g.at[q, :, :, LO, col(LANE - LANE * y, LANE)], x3gl.at[t], here.to_y),
            (x2i.at[q, :, :, LO, col(LANE - LANE * x, LANE)], x3il.at[t], here.to_x),
            (x2g.at[q, :, 1 - zn, HI], x3gh.at[t], here.to_zn),
            (x2i.at[q, :, 1 - zn, HI], x3ih.at[t], here.to_zn),
            (x2o.at[q, :, LO, col(WIDE - WIDE * x, WIDE)], x3a.at[t], here.to_x),
            (x2o.at[q, :, HI, col(WIDE - WIDE * y, WIDE)], x3b.at[t], here.to_y),
        ))

    def q4(b):
        taken(3, b)
        o, q, t = slot_of(2, b), slot_of(3, b), slot_of(4, b)
        for f in range(2):
            for k in range(2):
                x3gl[q, f, k] += x2g[o, f, k, LO, col(LANE * y, LANE)]
                x3il[q, f, k] += x2i[o, f, k, LO, col(LANE * x, LANE)]
            x3gh[q, f] += x2g[o, f, zn, HI]
            x3ih[q, f] += x2i[o, f, zn, HI]
            x3a[q, f] += x2o[o, f, LO, col(WIDE * x, WIDE)]
            x3b[q, f] += x2o[o, f, HI, col(WIDE * y, WIDE)]
        push(4, b, (
            (x3gl.at[q, :, 1 - zn], x4g.at[t, :, LO], here.to_zn),
            (x3il.at[q, :, 1 - zn], x4i.at[t, :, LO], here.to_zn),
            (x3gh.at[q, :, :, col(LANE - LANE * y, LANE)], x4g.at[t, :, HI], here.to_y),
            (x3ih.at[q, :, :, col(LANE - LANE * x, LANE)], x4i.at[t, :, HI], here.to_x),
            (x3a.at[q, :, :, col(LANE - LANE * y, LANE)], x4a.at[t], here.to_y),
            (x3b.at[q, :, :, col(LANE - LANE * x, LANE)], x4b.at[t], here.to_x),
        ))

    def q5(b):
        taken(4, b)
        o, q, t = slot_of(3, b), slot_of(4, b), slot_of(5, b)
        for f in range(2):
            x4g[q, f, LO] += x3gl[o, f, zn]
            x4i[q, f, LO] += x3il[o, f, zn]
            x4g[q, f, HI] += x3gh[o, f, :, col(LANE * y, LANE)]
            x4i[q, f, HI] += x3ih[o, f, :, col(LANE * x, LANE)]
            x4a[q, f] += x3a[o, f, :, col(LANE * y, LANE)]
            x4b[q, f] += x3b[o, f, :, col(LANE * x, LANE)]
        push(5, b, (
            (x4g.at[q, 1 - zf], x5g.at[t], here.to_zf),
            (x4i.at[q, 1 - zf], x5i.at[t], here.to_zf),
            (x4a.at[q, 1 - zf], x5a.at[t], here.to_zf),
            (x4b.at[q, 1 - zf], x5b.at[t], here.to_zf),
        ))

    def q6(b):
        taken(5, b)
        o, q = slot_of(4, b), slot_of(5, b)
        c = n_block - 1 - b
        v, p = c // n_stage, c % n_stage
        t = b % F_SLOTS

        @pl.when(b >= F_SLOTS)
        def _():
            wait_bytes(g_total(5), own.at[t])

        fg[t] = x5g[q] + x4g[o, zf]
        fi[t] = x5i[q] + x4i[o, zf]
        fa[t] = x5a[q] + x4a[o, zf]
        fb[t] = x5b[q] + x4b[o, zf]
        moves = (
            (fg.at[t], gg.at[v, 0, :, col(c_g, LANE)]),
            (fi.at[t], gi.at[v, 0, :, col(c_i, LANE)]),
            (fa.at[t], go.at[v, 0, pl.ds(pl.multiple_of(PIECE * (2 * core + x), SUB), SUB), col(LANE * y, LANE)]),
            (fb.at[t], go.at[v, 0, pl.ds(pl.multiple_of(PIECE * (2 * core + y) + SUB, SUB), SUB), col(LANE * x, LANE)]),
        )

        @pl.when(p == s)
        def _():
            for src, dst in moves:
                pltpu.make_async_copy(src, dst, own.at[t]).start()

        @pl.when(p != s)
        def _():
            for src, dst in moves:
                remote(src, dst, own.at[t], fsem.at[v], (z, p)).start()

    def bwd_tile(b, i):
        at = pl.ds(pl.multiple_of(i * tile, tile), tile)
        p, c = b % 2, n_block - 1 - b
        first = i == 0
        x32 = h[c % H_SLOTS, at, :].astype(F32)
        inv = lax.rsqrt(jnp.mean(x32 * x32, axis=-1, keepdims=True) + NORM_EPS)
        hr = x32 * inv
        n = hr.astype(BF16)
        et = e[0, at, :]
        q = jnp.zeros((tile, WIDE), F32)

        def add(m, k, value):
            for f in range(2):
                for r in range(2):
                    part = value[LANE * f + PIECE * r : LANE * f + PIECE * r + PIECE]
                    old = g[p, m, f, r, :, WIDE * k : WIDE * k + WIDE]
                    g[p, m, f, r, :, WIDE * k : WIDE * k + WIDE] = part + jnp.where(first, 0.0, old)

        def up(k):
            return mat(n, square(w, c, 0, k)), mat(n, square(w, c, 1, k)), mat_cols(et, out_square(w, c, k))

        ahead = up(0)
        for k in range(4):
            a, bb, t = ahead
            if k < 3:
                ahead = up(k + 1)
            sg = jax.nn.sigmoid(a)
            act = a * sg
            u = (act * bb).astype(BF16)
            da = (t * bb * sg * (1.0 + a * (1.0 - sg))).astype(BF16)
            db = (t * act).astype(BF16)
            q += mat_cols(da, square(w, c, 0, k)) + mat_cols(db, square(w, c, 1, k))
            add(0, k, mat_rows(n, da))
            add(1, k, mat_rows(n, db))
            do = mat_rows(u, et)
            for j in range(4):
                old = g[p, 2, k // 2, k % 2, :, WIDE * j : WIDE * j + WIDE]
                g[p, 2, k // 2, k % 2, :, WIDE * j : WIDE * j + WIDE] = do[PIECE * j : PIECE * j + PIECE] + jnp.where(first, 0.0, old)
        grad = et.astype(F32) + inv * (q - hr * jnp.mean(q * hr, axis=-1, keepdims=True))
        e[0, at, :] = grad.astype(BF16)

    def drain_step(i, carry):
        for k, fn in ((6, q6), (5, q5), (4, q4), (3, q3), (2, q2), (1, q1)):
            since = i - Q_AT[k]

            @pl.when((since >= 0) & (since < span) & ((since + span) % TICKS == 0))
            def _(fn=fn, since=since):
                fn(since // TICKS)

        return carry

    def bwd_step(i, carry):
        drain_step(i, carry)
        b = i // TICKS
        c = n_block - 1 - b

        @pl.when(i % TICKS == 0)
        def _():
            @pl.when(c < n_kept)
            def _():
                recall(c).wait()

            @pl.when((c - 2 >= 0) & (c - 2 < n_kept))
            def _():
                recall(c - 2).start()

        bwd_tile(b, i % TICKS)
        return carry

    half = rows // 2
    lo, hi = pl.ds(0, half), pl.ds(half, half)

    def share(k, src, dst, part, to):
        return remote(e.at[src, part], e.at[dst, part], as_.at[k], ar.at[k], to)

    shares = (
        share(0, 0, 1, lo, here.to_x),
        share(1, 0, 2, hi, here.to_y),
        share(2, 0, 2, lo, here.to_y),
        share(3, 0, 1, hi, here.to_x),
        share(4, 2, 3, hi, here.to_x),
        share(5, 1, 3, lo, here.to_y),
    )
    needs = {4: 1, 5: 0}
    at_tick = 0
    for k, share_at in enumerate(SHARE_AT):
        lax.fori_loop(at_tick, span + share_at, bwd_step if share_at <= 0 else drain_step, 0)
        at_tick = span + share_at
        if k in needs:
            shares[needs[k]].wait_recv()
        shares[k].start()
    lax.fori_loop(at_tick, span + max(Q_AT), drain_step, 0)

    own_slots = (s, here.to_x[1], here.to_y[1], 2 * (n_stage // 2 - 1 - s // 2) + core)
    hands = []
    for k, slot in enumerate(own_slots):
        hands.append(remote(e.at[k], ga.at[slot], cs.at[k], cr.at[k], here.to_core))
        hands.append(pltpu.make_async_copy(e.at[k], ga.at[slot], cl.at[k]))
    for k in range(4):
        for j in ((), (3,), (2,), (4, 5))[k]:
            shares[j].wait_recv()
        for copy in hands[2 * k : 2 * k + 2]:
            copy.start()
    for copy in shares:
        copy.wait_send()

    def finish(t, carry):
        wait_bytes(g_total(5), own.at[t])
        return carry

    lax.fori_loop(0, F_SLOTS, finish, 0)
    for v in range(n_v):
        wait_bytes(w.at[0, :, 0, 0, :, 0 : LANE * (n_stage - 1)], s0.at[v])
        wait_bytes(g.at[0, :, 0, 0, :, 0 : LANE * (n_stage - 1)], fsem.at[v])
    for copy in hands:
        copy.wait()


def settle_kernel(*refs):
    n = (len(refs) - 2) // 3
    srcs, dsts, bufs, (rsem, wsem) = refs[:n], refs[n : 2 * n], refs[2 * n : 3 * n], refs[3 * n :]
    moves = []
    for a in range(n):
        for i in range(srcs[a].shape[0]):
            k = len(moves)
            moves.append((
                pltpu.make_async_copy(srcs[a].at[i], bufs[a].at[i], rsem.at[k]),
                pltpu.make_async_copy(bufs[a].at[i], dsts[a].at[i], wsem.at[k]),
            ))
    for read, _ in moves:
        read.start()
    for read, write in moves:
        read.wait()
        write.start()
    for _, write in moves:
        write.wait()


def solution(mesh):
    n_stage = mesh.shape["stage"]
    act_spec = P(None, "data", None, None)
    w_spec = P(None, "stage", "data", None)
    hbm = pl.BlockSpec(memory_space=pltpu.HBM)
    dma = pltpu.SemaphoreType.DMA

    def body(act_in, cot_out, w_gate, w_in, w_out):
        n_micro, n_seq, n_tok, width = act_in.shape
        n_v, _, _, ffn = w_gate.shape
        n_block = n_v * n_stage
        rows = n_micro // n_stage * n_seq * n_tok
        block = (3, 2, 2, PIECE, ffn)
        flops = 2 * rows * width * ffn * n_block

        def f32(*shape):
            return pltpu.VMEM(shape, F32)

        def bf16(*shape):
            return pltpu.VMEM(shape, BF16)

        _, n1, n2, n3, n4, n5 = Q_SLOTS
        results = (
            jax.ShapeDtypeStruct(w_gate.shape, F32),
            jax.ShapeDtypeStruct(w_in.shape, F32),
            jax.ShapeDtypeStruct(w_out.shape, F32),
            jax.ShapeDtypeStruct((n_stage, rows, width), BF16),
        )
        *done, _ = pl.pallas_call(
            functools.partial(step_kernel, n_stage),
            name="step",
            out_shape=(*results, jax.ShapeDtypeStruct((n_block - H_SLOTS, rows, width), BF16)),
            in_specs=[hbm] * 5,
            out_specs=[hbm] * 5,
            scratch_shapes=[
                bf16(n_block, *block),
                bf16(H_SLOTS, rows, width),
                bf16(4, rows, width),
                f32(2, *block),
                f32(n1, 3, 2, 2, PIECE, HALF),
                f32(n2, 2, 2, PIECE, WIDE),
                f32(n2, 2, 2, PIECE, WIDE),
                f32(n2, 2, PIECE, HALF),
                f32(n3, 2, 2, SUB, LANE),
                f32(n3, 2, 2, SUB, LANE),
                f32(n3, 2, SUB, WIDE),
                f32(n3, 2, SUB, WIDE),
                f32(n3, 2, SUB, WIDE),
                f32(n3, 2, SUB, WIDE),
                f32(n4, 2, PIECE, LANE),
                f32(n4, 2, PIECE, LANE),
                f32(n4, 2, SUB, LANE),
                f32(n4, 2, SUB, LANE),
                f32(n5, PIECE, LANE),
                f32(n5, PIECE, LANE),
                f32(n5, SUB, LANE),
                f32(n5, SUB, LANE),
                f32(F_SLOTS, PIECE, LANE),
                f32(F_SLOTS, PIECE, LANE),
                f32(F_SLOTS, SUB, LANE),
                f32(F_SLOTS, SUB, LANE),
                dma((n_v,)),
                dma((n_block,)),
                dma((5, P_SLOTS)),
                dma((5, P_SLOTS)),
                dma((5, max(Q_SLOTS))),
                dma((5, max(Q_SLOTS))),
                dma((F_SLOTS,)),
                dma((n_v,)),
                dma((n_block,)),
                dma((2,)),
                dma((6,)),
                dma((6,)),
                dma((4,)),
                dma((4,)),
                dma((4,)),
            ],
            compiler_params=pltpu.CompilerParams(collective_id=0, has_side_effects=True, vmem_limit_bytes=67_000_000),
            cost_estimate=pl.CostEstimate(flops=11 * flops, bytes_accessed=2**26, transcendentals=0),
        )(act_in.reshape(n_stage, rows, width), cot_out.reshape(n_stage, rows, width), w_gate, w_in, w_out)
        moved = sum(a.shape[0] for a in done)
        gg, gi, go, ga = pl.pallas_call(
            settle_kernel,
            name="settle",
            out_shape=results,
            in_specs=[hbm] * 4,
            out_specs=[hbm] * 4,
            scratch_shapes=[pltpu.VMEM(a.shape, a.dtype) for a in done] + [dma((moved,)), dma((moved,))],
        )(*done)
        return ga.reshape(act_in.shape), gg, gi, go

    return jax.shard_map(body, mesh=mesh, in_specs=(act_spec, act_spec, w_spec, w_spec, w_spec), out_specs=(act_spec, w_spec, w_spec, w_spec), check_vma=False)
```

time: 352 us -> 352 us (level)
    pallas_call x3 -> x2, Pallas kernels: 351 us -> 350 us  [the longest x1 344 us: body(): pl.pallas_call(functools.partial(step_kernel, n_stage), name='step', out_...]
where the time goes in v5:
time: 352 us; the launch traced here: 351 us
  Pallas kernels  350 us (99%)
    pallas_call x1, Pallas kernels, body(): pl.pallas_call(functools.partial(step_kernel, n_stage), name='step', out_...  344 us

profile of v5, /device:TPU:0, one launch (start us, length us, event | category | flops | bytes accessed | tf_op | source)
XLA Modules:
  0.0 351.0 jit_solution(4395040874141440901)
XLA Ops:
  0.6 344.3 %step.1 = (f32[2,1,64,1024]{3,2,1,0:T(8,128)}, f32[2,1,64,1024]{3,2,1,0:T(8,128)}, f32[2,1,256,256]{3,2,1,0:T(8,128)}, bf16[8,1536,256]{2,1,0:T(8,128)(2,1)}, bf16[13,1536,256]{2,1,0:T(8,128)(2,1)}) custom-call(bf16[8,1536,256]{2,1,0:T(8,128)(2,1)} %bitcast.3, bf16[8,1536,256]{2,1,0:T(8,128)(2,1)} %bitcast.4, bf16[2,1,64,1024]{3,2,1,0:T(8,128)(2,1)} %wg.1, ...), custom_call_target="tpu_custom_call" | custom-call | flops 141733920768 | bytes 67108864 | tf_op jit(solution)/shard_map/step/pallas_call | solution.py:526
  344.9 6.1 %settle.1 = (f32[2,1,64,1024]{3,2,1,0:T(8,128)}, f32[2,1,64,1024]{3,2,1,0:T(8,128)}, f32[2,1,256,256]{3,2,1,0:T(8,128)}, bf16[8,1536,256]{2,1,0:T(8,128)(2,1)}) custom-call(f32[2,1,64,1024]{3,2,1,0:T(8,128)} %get-tuple-element.12.refs_0_, f32[2,1,64,1024]{3,2,1,0:T(8,128)} %get-tuple-element.13.refs_1_, f32[2,1,256,256]{3,2,1,0:T(8,128)} %get-tuple-element.14.refs_2_, ...), custom_call_target="tpu_custom_call" | custom-call | tf_op jit(solution)/shard_map/settle/pallas_call | solution.py:579

commit v6 on v5

--- a/solution.py
+++ b/solution.py
@@ -12,14 +12,15 @@
 TICKS = 3
 H_SLOTS = 3
 F_SLOTS = 6
-P_SLOTS = 10
-P_AHEAD = (0, 20, 15, 11, 6, 3)
+P_AHEAD = (0, 19, 14, 10, 5, 2)
 Q_SLOTS = (0, 4, 7, 9, 9, 8)
-Q_AT = (0, 3, 5, 10, 18, 26, 36)
-SHARE_AT = (-1, 0, 2, 3, 17, 20)
+Q_AT = (0, 3, 5, 10, 19, 27, 37)
+RELAY_AT = 7
+HAND_AT = 10
 LANE, WIDE, HALF = 128, 256, 512
 PIECE, SUB = 64, 32
 LO, HI = slice(0, SUB), slice(SUB, PIECE)
+MOST, REST = slice(0, 48), slice(48, PIECE)
 F32 = jnp.float32
 BF16 = jnp.bfloat16
 
@@ -87,7 +88,6 @@
     n_v = n_block // n_stage
     rows = h.shape[1]
     tile = rows // TICKS
-    span = TICKS * n_block
     c_g, c_i = narrow(core, x, y), narrow(core, y, x)
     c_x, c_y, c_c = narrow(core, x, 0), narrow(core, y, 0), narrow(core, 0, 0)
 
@@ -128,15 +128,19 @@
             )
         if phase == 2:
             return (
-                (w.at[c, 0, :, zn, :, col(c_g, LANE)], here.to_zn),
-                (w.at[c, 1, :, zn, :, col(c_i, LANE)], here.to_zn),
+                (w.at[c, 0, :, zn, MOST, col(c_g, LANE)], here.to_zn),
+                (w.at[c, 0, :, zn, REST, col(c_g, LANE)], here.to_y),
+                (w.at[c, 1, :, zn, MOST, col(c_i, LANE)], here.to_zn),
+                (w.at[c, 1, :, zn, REST, col(c_i, LANE)], here.to_x),
                 (w.at[c, 2, :, zn, 0:SUB, col(c_g, LANE)], here.to_y),
                 (w.at[c, 2, :, zn, SUB:PIECE, col(c_i, LANE)], here.to_x),
             )
         if phase == 3:
             return (
-                (w.at[c, 0, :, :, :, col(c_g, LANE)], here.to_y),
-                (w.at[c, 1, :, :, :, col(c_i, LANE)], here.to_x),
+                (w.at[c, 0, :, :, MOST, col(c_g, LANE)], here.to_y),
+                (w.at[c, 0, :, zn, REST, col(c_x, WIDE)], here.to_zn),
+                (w.at[c, 1, :, :, MOST, col(c_i, LANE)], here.to_x),
+                (w.at[c, 1, :, zn, REST, col(c_y, WIDE)], here.to_zn),
                 (w.at[c, 2, :, zn, 0:SUB, col(c_x, WIDE)], here.to_x),
                 (w.at[c, 2, :, zn, SUB:PIECE, col(c_y, WIDE)], here.to_y),
             )
@@ -159,18 +163,16 @@
         if phase == 0:
             wait_bytes(w_total(1, c), r0.at[c])
         else:
-            slot = c % P_SLOTS
-            wait_bytes(w_total(phase, c), pr.at[phase - 1, slot])
-            wait_bytes(w_total(phase, c), ps.at[phase - 1, slot])
+            wait_bytes(w_total(phase, c), pr.at[phase - 1, c])
+            wait_bytes(w_total(phase, c), ps.at[phase - 1, c])
 
     def advance(phase, c):
         arrived(phase - 1, c)
-        slot = c % P_SLOTS
         for ref, to in parts(phase, c):
-            remote(ref, ref, ps.at[phase - 1, slot], pr.at[phase - 1, slot], to).start()
+            remote(ref, ref, ps.at[phase - 1, c], pr.at[phase - 1, c], to).start()
 
     def fwd_tile(c, i):
-        at = pl.ds(pl.multiple_of(i * tile, tile), tile)
+        at = slice(i * tile, i * tile + tile)
         x32 = h[c % H_SLOTS, at, :].astype(F32)
         inv = lax.rsqrt(jnp.mean(x32 * x32, axis=-1, keepdims=True) + NORM_EPS)
         n = (x32 * inv).astype(BF16)
@@ -191,44 +193,45 @@
         return pltpu.make_async_copy(h_all.at[c], h.at[c % H_SLOTS], hsem.at[c])
 
     n_kept = n_block - H_SLOTS
-    lead = max(P_AHEAD)
+    lead = (max(P_AHEAD) + TICKS - 1) // TICKS
+
+    def gather(j, r):
+        for k in (5, 4, 3, 2, 1):
+            if (P_AHEAD[k] + r) % TICKS == 0:
+                c = j + (P_AHEAD[k] + r) // TICKS
+
+                @pl.when((c >= 0) & (c < n_block))
+                def _(k=k, c=c):
+                    advance(k, c)
 
     def lead_step(i, carry):
-        for k in (5, 4, 3, 2, 1):
-            since = i - lead + P_AHEAD[k]
-
-            @pl.when((since >= 0) & (since < span) & ((since + TICKS * lead) % TICKS == 0))
-            def _(k=k, since=since):
-                advance(k, since // TICKS)
-
+        for r in range(TICKS):
+            gather(i - lead, r)
         return carry
 
-    def fwd_step(i, carry):
-        lead_step(i, carry)
-        now = i - lead
-        c = now // TICKS
-
-        @pl.when(now % TICKS == 0)
-        def _():
-            arrived(5, c)
-
-            @pl.when((c >= 2) & (c - 2 < n_kept))
-            def _():
-                keep(c - 2).wait()
-
-        @pl.when((now % TICKS == 1) & (c < n_kept))
-        def _():
-            keep(c).start()
-
-        @pl.when(c < n_block - 1)
-        def _():
-            fwd_tile(c, now % TICKS)
-
+    def fwd_step(c, carry):
+        for r in range(TICKS):
+            gather(c, r)
+            if r == 0:
+                arrived(5, c)
+
+                @pl.when((c >= 2) & (c - 2 < n_kept))
+                def _():
+                    keep(c - 2).wait()
+
+            if r == 1:
+
+                @pl.when(c < n_kept)
+                def _():
+                    keep(c).start()
+
+            fwd_tile(c, r)
         return carry
 
     lax.fori_loop(0, lead, lead_step, 0)
     load_h.wait()
-    lax.fori_loop(lead, lead + span, fwd_step, 0)
+    lax.fori_loop(0, n_block - 1, fwd_step, 0)
+    arrived(5, n_block - 1)
     load_e.wait()
 
     def g_total(phase):
@@ -358,9 +361,8 @@
                 remote(src, dst, own.at[t], fsem.at[v], (z, p)).start()
 
     def bwd_tile(b, i):
-        at = pl.ds(pl.multiple_of(i * tile, tile), tile)
+        at = slice(i * tile, i * tile + tile)
         p, c = b % 2, n_block - 1 - b
-        first = i == 0
         x32 = h[c % H_SLOTS, at, :].astype(F32)
         inv = lax.rsqrt(jnp.mean(x32 * x32, axis=-1, keepdims=True) + NORM_EPS)
         hr = x32 * inv
@@ -372,8 +374,9 @@
             for f in range(2):
                 for r in range(2):
                     part = value[LANE * f + PIECE * r : LANE * f + PIECE * r + PIECE]
-                    old = g[p, m, f, r, :, WIDE * k : WIDE * k + WIDE]
-                    g[p, m, f, r, :, WIDE * k : WIDE * k + WIDE] = part + jnp.where(first, 0.0, old)
+                    if i > 0:
+                        part += g[p, m, f, r, :, WIDE * k : WIDE * k + WIDE]
+                    g[p, m, f, r, :, WIDE * k : WIDE * k + WIDE] = part
 
         def up(k):
             return mat(n, square(w, c, 0, k)), mat(n, square(w, c, 1, k)), mat_cols(et, out_square(w, c, k))
@@ -393,37 +396,42 @@
             add(1, k, mat_rows(n, db))
             do = mat_rows(u, et)
             for j in range(4):
-                old = g[p, 2, k // 2, k % 2, :, WIDE * j : WIDE * j + WIDE]
-                g[p, 2, k // 2, k % 2, :, WIDE * j : WIDE * j + WIDE] = do[PIECE * j : PIECE * j + PIECE] + jnp.where(first, 0.0, old)
+                part = do[PIECE * j : PIECE * j + PIECE]
+                if i > 0:
+                    part += g[p, 2, k // 2, k % 2, :, WIDE * j : WIDE * j + WIDE]
+                g[p, 2, k // 2, k % 2, :, WIDE * j : WIDE * j + WIDE] = part
         grad = et.astype(F32) + inv * (q - hr * jnp.mean(q * hr, axis=-1, keepdims=True))
         e[0, at, :] = grad.astype(BF16)
 
-    def drain_step(i, carry):
+    def scatter_sums(j, r):
         for k, fn in ((6, q6), (5, q5), (4, q4), (3, q3), (2, q2), (1, q1)):
-            since = i - Q_AT[k]
-
-            @pl.when((since >= 0) & (since < span) & ((since + span) % TICKS == 0))
-            def _(fn=fn, since=since):
-                fn(since // TICKS)
-
+            if Q_AT[k] % TICKS == r:
+                b = j - Q_AT[k] // TICKS
+
+                @pl.when((b >= 0) & (b < n_block))
+                def _(fn=fn, b=b):
+                    fn(b)
+
+    def drain_step(j, carry):
+        for r in range(TICKS):
+            scatter_sums(j, r)
         return carry
 
-    def bwd_step(i, carry):
-        drain_step(i, carry)
-        b = i // TICKS
+    def bwd_step(b, carry):
         c = n_block - 1 - b
-
-        @pl.when(i % TICKS == 0)
-        def _():
-            @pl.when(c < n_kept)
-            def _():
-                recall(c).wait()
-
-            @pl.when((c - 2 >= 0) & (c - 2 < n_kept))
-            def _():
-                recall(c - 2).start()
-
-        bwd_tile(b, i % TICKS)
+        for r in range(TICKS):
+            scatter_sums(b, r)
+            if r == 0:
+
+                @pl.when(c < n_kept)
+                def _():
+                    recall(c).wait()
+
+                @pl.when((c - 2 >= 0) & (c - 2 < n_kept))
+                def _():
+                    recall(c - 2).start()
+
+            bwd_tile(b, r)
         return carry
 
     half = rows // 2
@@ -434,32 +442,40 @@
 
     shares = (
         share(0, 0, 1, lo, here.to_x),
-        share(1, 0, 2, hi, here.to_y),
-        share(2, 0, 2, lo, here.to_y),
+        share(1, 0, 2, lo, here.to_y),
+        share(2, 0, 2, hi, here.to_y),
         share(3, 0, 1, hi, here.to_x),
-        share(4, 2, 3, hi, here.to_x),
-        share(5, 1, 3, lo, here.to_y),
+        share(4, 1, 3, lo, here.to_y),
+        share(5, 2, 3, hi, here.to_x),
     )
-    needs = {4: 1, 5: 0}
-    at_tick = 0
-    for k, share_at in enumerate(SHARE_AT):
-        lax.fori_loop(at_tick, span + share_at, bwd_step if share_at <= 0 else drain_step, 0)
-        at_tick = span + share_at
-        if k in needs:
-            shares[needs[k]].wait_recv()
-        shares[k].start()
-    lax.fori_loop(at_tick, span + max(Q_AT), drain_step, 0)
-
+    needs = {4: 0, 5: 2}
     own_slots = (s, here.to_x[1], here.to_y[1], 2 * (n_stage // 2 - 1 - s // 2) + core)
     hands = []
     for k, slot in enumerate(own_slots):
         hands.append(remote(e.at[k], ga.at[slot], cs.at[k], cr.at[k], here.to_core))
         hands.append(pltpu.make_async_copy(e.at[k], ga.at[slot], cl.at[k]))
-    for k in range(4):
-        for j in ((), (3,), (2,), (4, 5))[k]:
-            shares[j].wait_recv()
+
+    def hand(k):
         for copy in hands[2 * k : 2 * k + 2]:
             copy.start()
+
+    lax.fori_loop(0, n_block, bwd_step, 0)
+    for copy in shares[:4]:
+        copy.start()
+    hand(0)
+    lax.fori_loop(n_block, n_block + RELAY_AT, drain_step, 0)
+    for k in needs:
+        shares[needs[k]].wait_recv()
+        shares[k].start()
+    lax.fori_loop(n_block + RELAY_AT, n_block + HAND_AT, drain_step, 0)
+    shares[3].wait_recv()
+    hand(1)
+    shares[1].wait_recv()
+    hand(2)
+    lax.fori_loop(n_block + HAND_AT, n_block + max(Q_AT) // TICKS + 1, drain_step, 0)
+    shares[4].wait_recv()
+    shares[5].wait_recv()
+    hand(3)
     for copy in shares:
         copy.wait_send()
 
@@ -558,8 +574,8 @@
                 f32(F_SLOTS, SUB, LANE),
                 dma((n_v,)),
                 dma((n_block,)),
-                dma((5, P_SLOTS)),
-                dma((5, P_SLOTS)),
+                dma((5, n_block)),
+                dma((5, n_block)),
                 dma((5, max(Q_SLOTS))),
                 dma((5, max(Q_SLOTS))),
                 dma((F_SLOTS,)),

time: 352 us -> 345 us (0.980)
  Pallas kernels: 350 us -> 344 us
    pallas_call x1, Pallas kernels: 344 us -> 338 us  [body(): pl.pallas_call(functools.partial(step_kernel, n_stage), name='step', out_...]
where the time goes in v6:
time: 345 us; the launch traced here: 344 us
  Pallas kernels  344 us (100%)
    pallas_call x1, Pallas kernels, body(): pl.pallas_call(functools.partial(step_kernel, n_stage), name='step', out_...  338 us

profile of v6, /device:TPU:0, one launch (start us, length us, event | category | flops | bytes accessed | tf_op | source)
XLA Modules:
  0.0 344.4 jit_solution(17145770773726230187)
XLA Ops:
  0.6 337.6 %step.1 = (f32[2,1,64,1024]{3,2,1,0:T(8,128)}, f32[2,1,64,1024]{3,2,1,0:T(8,128)}, f32[2,1,256,256]{3,2,1,0:T(8,128)}, bf16[8,1536,256]{2,1,0:T(8,128)(2,1)}, bf16[13,1536,256]{2,1,0:T(8,128)(2,1)}) custom-call(bf16[8,1536,256]{2,1,0:T(8,128)(2,1)} %bitcast.3, bf16[8,1536,256]{2,1,0:T(8,128)(2,1)} %bitcast.4, bf16[2,1,64,1024]{3,2,1,0:T(8,128)(2,1)} %wg.1, ...), custom_call_target="tpu_custom_call" | custom-call | flops 141733920768 | bytes 67108864 | tf_op jit(solution)/shard_map/step/pallas_call | solution.py:542
  338.2 6.1 %settle.1 = (f32[2,1,64,1024]{3,2,1,0:T(8,128)}, f32[2,1,64,1024]{3,2,1,0:T(8,128)}, f32[2,1,256,256]{3,2,1,0:T(8,128)}, bf16[8,1536,256]{2,1,0:T(8,128)(2,1)}) custom-call(f32[2,1,64,1024]{3,2,1,0:T(8,128)} %get-tuple-element.12.refs_0_, f32[2,1,64,1024]{3,2,1,0:T(8,128)} %get-tuple-element.13.refs_1_, f32[2,1,256,256]{3,2,1,0:T(8,128)} %get-tuple-element.14.refs_2_, ...), custom_call_target="tpu_custom_call" | custom-call | tf_op jit(solution)/shard_map/settle/pallas_call | solution.py:595

commit v7 on v6

--- a/solution.py
+++ b/solution.py
@@ -20,7 +20,6 @@
 LANE, WIDE, HALF = 128, 256, 512
 PIECE, SUB = 64, 32
 LO, HI = slice(0, SUB), slice(SUB, PIECE)
-MOST, REST = slice(0, 48), slice(48, PIECE)
 F32 = jnp.float32
 BF16 = jnp.bfloat16
 
@@ -128,19 +127,15 @@
             )
         if phase == 2:
             return (
-                (w.at[c, 0, :, zn, MOST, col(c_g, LANE)], here.to_zn),
-                (w.at[c, 0, :, zn, REST, col(c_g, LANE)], here.to_y),
-                (w.at[c, 1, :, zn, MOST, col(c_i, LANE)], here.to_zn),
-                (w.at[c, 1, :, zn, REST, col(c_i, LANE)], here.to_x),
+                (w.at[c, 0, :, zn, :, col(c_g, LANE)], here.to_zn),
+                (w.at[c, 1, :, zn, :, col(c_i, LANE)], here.to_zn),
                 (w.at[c, 2, :, zn, 0:SUB, col(c_g, LANE)], here.to_y),
                 (w.at[c, 2, :, zn, SUB:PIECE, col(c_i, LANE)], here.to_x),
             )
         if phase == 3:
             return (
-                (w.at[c, 0, :, :, MOST, col(c_g, LANE)], here.to_y),
-                (w.at[c, 0, :, zn, REST, col(c_x, WIDE)], here.to_zn),
-                (w.at[c, 1, :, :, MOST, col(c_i, LANE)], here.to_x),
-                (w.at[c, 1, :, zn, REST, col(c_y, WIDE)], here.to_zn),
+                (w.at[c, 0, :, :, :, col(c_g, LANE)], here.to_y),
+                (w.at[c, 1, :, :, :, col(c_i, LANE)], here.to_x),
                 (w.at[c, 2, :, zn, 0:SUB, col(c_x, WIDE)], here.to_x),
                 (w.at[c, 2, :, zn, SUB:PIECE, col(c_y, WIDE)], here.to_y),
             )
@@ -404,7 +399,7 @@
         e[0, at, :] = grad.astype(BF16)
 
     def scatter_sums(j, r):
-        for k, fn in ((6, q6), (5, q5), (4, q4), (3, q3), (2, q2), (1, q1)):
+        for k, fn in ((1, q1), (6, q6), (5, q5), (4, q4), (3, q3), (2, q2)):
             if Q_AT[k] % TICKS == r:
                 b = j - Q_AT[k] // TICKS
 

time: 345 us -> 345 us (level)
  no operation moved by 1% of the time
where the time goes in v7:
time: 345 us
  Pallas kernels  344 us (100%)
    pallas_call x1, Pallas kernels, body(): pl.pallas_call(functools.partial(step_kernel, n_stage), name='step', out_...  338 us

profile of v7, /device:TPU:0, one launch (start us, length us, event | category | flops | bytes accessed | tf_op | source)
XLA Modules:
  0.0 345.1 jit_solution(5839252782612309825)
XLA Ops:
  0.6 338.3 %step.1 = (f32[2,1,64,1024]{3,2,1,0:T(8,128)}, f32[2,1,64,1024]{3,2,1,0:T(8,128)}, f32[2,1,256,256]{3,2,1,0:T(8,128)}, bf16[8,1536,256]{2,1,0:T(8,128)(2,1)}, bf16[13,1536,256]{2,1,0:T(8,128)(2,1)}) custom-call(bf16[8,1536,256]{2,1,0:T(8,128)(2,1)} %bitcast.3, bf16[8,1536,256]{2,1,0:T(8,128)(2,1)} %bitcast.4, bf16[2,1,64,1024]{3,2,1,0:T(8,128)(2,1)} %wg.1, ...), custom_call_target="tpu_custom_call" | custom-call | flops 141733920768 | bytes 67108864 | tf_op jit(solution)/shard_map/step/pallas_call | solution.py:537
  338.9 6.1 %settle.1 = (f32[2,1,64,1024]{3,2,1,0:T(8,128)}, f32[2,1,64,1024]{3,2,1,0:T(8,128)}, f32[2,1,256,256]{3,2,1,0:T(8,128)}, bf16[8,1536,256]{2,1,0:T(8,128)(2,1)}) custom-call(f32[2,1,64,1024]{3,2,1,0:T(8,128)} %get-tuple-element.12.refs_0_, f32[2,1,64,1024]{3,2,1,0:T(8,128)} %get-tuple-element.13.refs_1_, f32[2,1,256,256]{3,2,1,0:T(8,128)} %get-tuple-element.14.refs_2_, ...), custom_call_target="tpu_custom_call" | custom-call | tf_op jit(solution)/shard_map/settle/pallas_call | solution.py:590

commit v8 on v6

--- a/solution.py
+++ b/solution.py
@@ -12,7 +12,7 @@
 TICKS = 3
 H_SLOTS = 3
 F_SLOTS = 6
-P_AHEAD = (0, 19, 14, 10, 5, 2)
+P_AHEAD = (0, 20, 15, 11, 5, 2)
 Q_SLOTS = (0, 4, 7, 9, 9, 8)
 Q_AT = (0, 3, 5, 10, 19, 27, 37)
 RELAY_AT = 7
@@ -404,7 +404,7 @@
         e[0, at, :] = grad.astype(BF16)
 
     def scatter_sums(j, r):
-        for k, fn in ((6, q6), (5, q5), (4, q4), (3, q3), (2, q2), (1, q1)):
+        for k, fn in ((1, q1), (6, q6), (5, q5), (4, q4), (3, q3), (2, q2)):
             if Q_AT[k] % TICKS == r:
                 b = j - Q_AT[k] // TICKS
 

time: 345 us -> 347 us (level)
  no operation moved by 1% of the time
where the time goes in v8:
time: 347 us
  Pallas kernels  346 us (100%)
    pallas_call x1, Pallas kernels, body(): pl.pallas_call(functools.partial(step_kernel, n_stage), name='step', out_...  340 us

profile of v8, /device:TPU:0, one launch (start us, length us, event | category | flops | bytes accessed | tf_op | source)
XLA Modules:
  0.0 346.6 jit_solution(12628433558086342831)
XLA Ops:
  0.6 339.8 %step.1 = (f32[2,1,64,1024]{3,2,1,0:T(8,128)}, f32[2,1,64,1024]{3,2,1,0:T(8,128)}, f32[2,1,256,256]{3,2,1,0:T(8,128)}, bf16[8,1536,256]{2,1,0:T(8,128)(2,1)}, bf16[13,1536,256]{2,1,0:T(8,128)(2,1)}) custom-call(bf16[8,1536,256]{2,1,0:T(8,128)(2,1)} %bitcast.3, bf16[8,1536,256]{2,1,0:T(8,128)(2,1)} %bitcast.4, bf16[2,1,64,1024]{3,2,1,0:T(8,128)(2,1)} %wg.1, ...), custom_call_target="tpu_custom_call" | custom-call | flops 141733920768 | bytes 67108864 | tf_op jit(solution)/shard_map/step/pallas_call | solution.py:542
  340.4 6.1 %settle.1 = (f32[2,1,64,1024]{3,2,1,0:T(8,128)}, f32[2,1,64,1024]{3,2,1,0:T(8,128)}, f32[2,1,256,256]{3,2,1,0:T(8,128)}, bf16[8,1536,256]{2,1,0:T(8,128)(2,1)}) custom-call(f32[2,1,64,1024]{3,2,1,0:T(8,128)} %get-tuple-element.12.refs_0_, f32[2,1,64,1024]{3,2,1,0:T(8,128)} %get-tuple-element.13.refs_1_, f32[2,1,256,256]{3,2,1,0:T(8,128)} %get-tuple-element.14.refs_2_, ...), custom_call_target="tpu_custom_call" | custom-call | tf_op jit(solution)/shard_map/settle/pallas_call | solution.py:595
